TPU v7x, 128 devices: a whole 4x4x4 slice. The times are simulated.
128 devices in a mesh: team: 8 (over x, core), inner: 16 (over z, y).
Axes of the slice: x: 4, y: 4, z: 4, core: 2. Of those that a mesh axis runs over, the one named last changes fastest.
Arguments:
- queries: float32 [16384, 1024], P(('team', 'inner')), may hold values from -8 to 8
- passages: float32 [16384, 1024], P(('team', 'inner')), may hold values from -8 to 8
- positive: int32 [16384], P(('team', 'inner')), may hold values from 0 to 16383, as said below
Outputs:
- grad_queries: float32 [16384, 1024], P(('team', 'inner'))
- grad_passages: float32 [16384, 1024], P(('team', 'inner'))
Inputs may be any that keep to these rules, and one draw needn't show every extreme that they name: `positive`: a permutation of the passage indices 0 to 16383.
All inputs are finite; a program needn't handle non-finite values.
Results may differ from a plain program's by a relative error of at most 0.014.
Values may be sent and summed in bfloat16 or wider, within the bound.
A program may use at most 64 MiB of HBM per device.

v0:
```python
import jax
import jax.numpy as jnp
from jax import lax
from jax.sharding import Mesh
from jax.sharding import PartitionSpec as P

INNER = ("inner_0", "inner_1")
TEAM_INNER = ("team", "inner_0", "inner_1")


logit_scale_factor = 20.0
epsilon = 1e-06


def in_order(blocks, dim):
    dims = list(blocks.shape[1:])
    dims[dim] *= blocks.shape[0]
    return jnp.moveaxis(blocks, 0, dim).reshape(dims)


def sent_to_all(x, axis):
    copies = jnp.broadcast_to(x, (lax.axis_size(axis), *x.shape))
    return lax.all_to_all(copies, axis, split_axis=0, concat_axis=0, tiled=True)


def gathered_copies(x, axis, dim):
    return in_order(sent_to_all(x, axis), dim)


def taken_together(x, axis):
    everything = sent_to_all(x, axis)
    return jnp.sum(everything, axis=0)


def summed_rows(terms, axes):
    so_far = terms.astype(jnp.bfloat16)
    for axis in axes:
        so_far = lax.psum_scatter(so_far, axis, scatter_dimension=0, tiled=True)
    return so_far.astype(jnp.float32)


def split_up(x, dim, size):
    dims = x.shape
    blocks = x.reshape(*dims[:dim], size, dims[dim] // size, *dims[dim + 1 :])
    return jnp.moveaxis(blocks, dim, 0)


def summed_on_arrival(x, axis, dim):
    size = lax.axis_size(axis)
    blocks = lax.all_to_all(split_up(x, dim, size), axis, 0, 0, tiled=True)
    return jnp.sum(blocks.astype(jnp.float32), axis=0)


def unit_rows(vectors):
    length = jnp.sqrt(jnp.sum(vectors * vectors, axis=1, keepdims=True) + epsilon)
    return (vectors / length, length)


def finish(unit_vectors, length, grad_raw):
    projection = jnp.sum(unit_vectors * grad_raw, axis=1, keepdims=True)
    return (grad_raw - unit_vectors * projection) / length


def exponent(query_tile_rows, column_block):
    similarity_scores = lax.dot_general(
        query_tile_rows, column_block, (((1,), (1,)), ((), ())), preferred_element_type=jnp.float32
    )
    return jnp.exp(logit_scale_factor * similarity_scores)


def weights(query_tile_rows, column_block, target_block, row_block, column_block_total):
    exponentials = exponent(query_tile_rows, column_block)
    column_ids = lax.iota(jnp.int32, column_block.shape[0])
    is_target = (target_block[:, None] == column_ids[None, :]).astype(jnp.float32)
    combined = (
        exponentials / row_block[:, None]
        + exponentials / column_block_total[None, :]
        - 2.0 * is_target
    )
    return combined.astype(jnp.bfloat16)


def per_device(queries, passages, positive):
    shard_rows = queries.shape[0]
    feature_count = queries.shape[1]
    inner_count = lax.axis_size(INNER)
    team_count = lax.axis_size("team")
    query_unit, query_length = unit_rows(queries)
    passage_unit, passage_length = unit_rows(passages)
    query_round = query_unit.astype(jnp.bfloat16)
    passage_round = passage_unit.astype(jnp.bfloat16)
    team_queries = lax.all_gather(query_round, INNER, axis=0, tiled=True)
    team_targets = lax.all_gather(positive, INNER, axis=0, tiled=True)
    columns = gathered_copies(passage_round, "team", 0)
    team_rows = shard_rows * inner_count
    column_count = shard_rows * team_count
    owner_inner = team_targets % team_rows // shard_rows
    target_column = team_targets // team_rows * shard_rows + team_targets % shard_rows
    target_column = jnp.where(owner_inner == lax.axis_index(INNER), target_column, -1)
    block_rows = shard_rows * min(inner_count, max(1, 512 // shard_rows))
    block_count = team_rows // block_rows
    query_blocks = team_queries.reshape(block_count, block_rows, feature_count)

    def column_sums(running, query_tile_rows):
        exponentials = exponent(query_tile_rows, columns)
        return (running + jnp.sum(exponentials, axis=0), jnp.sum(exponentials, axis=1))

    column_part, row_parts = lax.scan(
        column_sums, jnp.zeros((column_count,), jnp.float32), query_blocks
    )
    row_total = taken_together(row_parts.reshape(team_rows), INNER)
    column_total = lax.psum(column_part, "team")
    query_tile_rows = team_queries
    loss_weight = weights(query_tile_rows, columns, target_column, row_total, column_total)
    query_grad = summed_rows(
        logit_scale_factor * jnp.dot(loss_weight, columns, preferred_element_type=jnp.float32),
        INNER,
    )
    loss_weight = weights(team_queries, columns, target_column, row_total, column_total)
    passage_grad = summed_on_arrival(
        (
            logit_scale_factor
            * lax.dot_general(
                loss_weight,
                team_queries,
                (((0,), (0,)), ((), ())),
                preferred_element_type=jnp.float32,
            )
        ).astype(jnp.bfloat16),
        "team",
        0,
    )
    grad_queries = finish(query_unit, query_length, query_grad)
    grad_passages = finish(passage_unit, passage_length, passage_grad)
    return (grad_queries, grad_passages)


def solution(mesh):
    finer = Mesh(mesh.devices.reshape(mesh.shape["team"], 4, 4), ("team", "inner_0", "inner_1"))
    in_specs = (P(TEAM_INNER, None), P(TEAM_INNER, None), P(TEAM_INNER))
    out_specs = (P(TEAM_INNER, None), P(TEAM_INNER, None))
    return jax.shard_map(
        per_device, mesh=finer, in_specs=in_specs, out_specs=out_specs, check_vma=False
    )
```

profile of v0, /device:TPU:0, one launch (start us, length us, event | category | flops | bytes accessed | tf_op | source)
XLA Modules:
  0.0 193.5 jit_solution(252195710733847977)
XLA Ops:
  7.2 1.2 multiply_reduce_fusion.2
  8.4 1.9 fusion.18
  10.3 1.2 multiply_reduce_fusion.1
  12.6 1.6 broadcast_in_dim.16
  14.2 4.4 %all-to-all-start = ((bf16[8,128,1024]{2,1,0:T(8,128)(2,1)}), bf16[8,128,1024]{2,1,0:T(8,128)(2,1)S(1)}, u32[]{:S(2)}, u32[]{:S(2)}) async-start(bf16[8,128,1024]{2,1,0:T(8,128)(2,1)} %broadcast_in_dim.16), calls=%async_computation | async-start | bytes 4194304 | tf_op jit(solution)/shard_map/all_to_all | solution.py:23
  18.6 22.2 %all-gather = s32[16,1,128]{2,1,0:T(1,128)S(1)} all-gather(s32[1,1,128]{2,1,0:T(1,128)S(1)} %bitcast.32), channel_id=1, replica_groups=mesh['team'=8,'inner_0'=4,'inner_1'=4] {'inner_0','inner_1'}, dimensions={0}, use_global_device_ids=true | all-gather | bytes 8704 | tf_op jit(solution)/shard_map/all_gather | solution.py:93
  40.8 5.0 %all-to-all-done = bf16[8,128,1024]{2,1,0:T(8,128)(2,1)S(1)} async-done(((bf16[8,128,1024]{2,1,0:T(8,128)(2,1)}), bf16[8,128,1024]{2,1,0:T(8,128)(2,1)S(1)}, u32[]{:S(2)}, u32[]{:S(2)}) %all-to-all-start) | async-done | bytes 2097184 | tf_op jit(solution)/shard_map/all_to_all | solution.py:23
  45.8 19.0 %all-gather.3.cloned.1.call-done = bf16[2048,1024]{1,0:T(8,128)(2,1)} async-done(((bf16[128,1024]{1,0:T(8,128)(2,1)}), bf16[2048,1024]{1,0:T(8,128)(2,1)}) %all-gather.3.cloned.1.call-update) | async-done | bytes 4194320 | tf_op jit(solution)/shard_map/all_gather | solution.py:92
  64.7 11.1 %while.13 = (s32[]{:T(128)}, f32[1024]{0:T(1024)S(1)}, f32[4,512]{1,0:T(4,128)S(1)}, bf16[4,512,1024]{2,1,0:T(8,128)(2,1)}, bf16[1024,1024]{1,0:T(8,128)(2,1)S(1)}, /*index=5*/s32[]{:T(128)}, s32[]{:T(128)}) while((s32[]{:T(128)}, f32[1024]{0:T(1024)S(1)}, f32[4,512]{1,0:T(4,128)S(1)}, bf16[4,512,1024]{2,1,0:T(8,128)(2,1)}, ...), condition=%wide.region_5.6_spmd.clone, body=%wide.region_2.5_spmd.clone.sunk | while | flops 1075315200 | bytes 3168359 | solution.py:108
  64.7 2.7 %fusion.29 = (f32[512]{0:T(512)S(1)}, f32[1024]{0:T(1024)S(1)}) fusion(bf16[1024,1024]{1,0:T(8,128)(2,1)S(1)} %get-tuple-element.115, bf16[4,512,1024]{2,1,0:T(8,128)(2,1)} %get-tuple-element.114, s32[]{:T(128)S(6)} %copy.12), kind=kOutput, calls=%fused_computation.1.clone.1 | convolution fusion | flops 1075313152 | bytes 3151876 | tf_op jit(solution)/shard_map/while/body/eval_jaxpr/dot_general | solution.py:65
  67.5 2.7 %fusion.29 = (f32[512]{0:T(512)S(1)}, f32[1024]{0:T(1024)S(1)}) fusion(bf16[1024,1024]{1,0:T(8,128)(2,1)S(1)} %get-tuple-element.115, bf16[4,512,1024]{2,1,0:T(8,128)(2,1)} %get-tuple-element.114, s32[]{:T(128)S(6)} %copy.12), kind=kOutput, calls=%fused_computation.1.clone.1 | convolution fusion | flops 1075313152 | bytes 3151876 | tf_op jit(solution)/shard_map/while/body/eval_jaxpr/dot_general | solution.py:65
  70.3 2.7 %fusion.29 = (f32[512]{0:T(512)S(1)}, f32[1024]{0:T(1024)S(1)}) fusion(bf16[1024,1024]{1,0:T(8,128)(2,1)S(1)} %get-tuple-element.115, bf16[4,512,1024]{2,1,0:T(8,128)(2,1)} %get-tuple-element.114, s32[]{:T(128)S(6)} %copy.12), kind=kOutput, calls=%fused_computation.1.clone.1 | convolution fusion | flops 1075313152 | bytes 3151876 | tf_op jit(solution)/shard_map/while/body/eval_jaxpr/dot_general | solution.py:65
  73.1 2.7 %fusion.29 = (f32[512]{0:T(512)S(1)}, f32[1024]{0:T(1024)S(1)}) fusion(bf16[1024,1024]{1,0:T(8,128)(2,1)S(1)} %get-tuple-element.115, bf16[4,512,1024]{2,1,0:T(8,128)(2,1)} %get-tuple-element.114, s32[]{:T(128)S(6)} %copy.12), kind=kOutput, calls=%fused_computation.1.clone.1 | convolution fusion | flops 1075313152 | bytes 3151876 | tf_op jit(solution)/shard_map/while/body/eval_jaxpr/dot_general | solution.py:65
  76.6 5.3 %all-to-all-start.1 = ((f32[16,1,2048]{2,1,0:T(1,128)}), f32[16,1,2048]{2,1,0:T(1,128)S(1)}, u32[]{:S(2)}, u32[]{:S(2)}) async-start(f32[16,1,2048]{2,1,0:T(1,128)} %broadcast_in_dim.36), calls=%async_computation.1 | async-start | bytes 262144 | tf_op jit(solution)/shard_map/all_to_all | solution.py:23
  82.0 14.4 %psum.7 = f32[1024]{0:T(1024)S(1)} all-reduce(f32[1024]{0:T(1024)S(1)} %get-tuple-element.31), channel_id=1, replica_groups=mesh['team'=8,'inner_0'=4,'inner_1'=4] {'team'}, use_global_device_ids=true, to_apply=%region_7.8 | all-reduce | flops 1024 | bytes 8192 | tf_op jit(solution)/shard_map/psum | solution.py:112
  96.5 7.9 %subtract_convert_fusion = bf16[2048,1024]{1,0:T(8,128)(2,1)S(1)} fusion(bf16[2048,1024]{1,0:T(8,128)(2,1)} %bitcast.34, bf16[1024,1024]{1,0:T(8,128)(2,1)S(1)} %get-tuple-element.125, s32[2048]{0:T(1024)S(1)} %fusion.12, f32[1024]{0:T(1024)S(1)} %psum.7, f32[2048]{0:T(1024)S(1)} %reduce_sum.74), kind=kOutput, calls=%fused_computation.9 | convolution fusion | flops 4311744512 | bytes 10506240 | tf_op jit(solution)/shard_map/dot_general | solution.py:65
  104.4 2.0 %copy-done.3 = bf16[2048,1024]{1,0:T(8,128)(2,1)} copy-done((bf16[2048,1024]{1,0:T(8,128)(2,1)}, bf16[2048,1024]{1,0:T(8,128)(2,1)S(1)}, u32[]{:S(2)}) %copy-start.3) | copy-done | bytes 4194328
  106.4 6.1 %multiply_convert_fusion = bf16[2048,1024]{1,0:T(8,128)(2,1)} fusion(bf16[2048,1024]{1,0:T(8,128)(2,1)S(1)} %subtract_convert_fusion, bf16[1024,1024]{1,0:T(8,128)(2,1)S(1)} %get-tuple-element.125), kind=kOutput, calls=%fused_computation.8 | convolution fusion | flops 4299161600 | bytes 10485760 | tf_op jit(solution)/shard_map/dot_general | solution.py:116
  112.5 9.4 %multiply_convert_fusion.1 = bf16[1024,1024]{1,0:T(8,128)(2,1)} fusion(bf16[2048,1024]{1,0:T(8,128)(2,1)} %copy-done.3, bf16[2048,1024]{1,0:T(8,128)(2,1)} %bitcast.35), kind=kOutput, calls=%fused_computation.12 | convolution fusion | flops 4297064448 | bytes 10485760 | tf_op jit(solution)/shard_map/dot_general | solution.py:123
  121.9 3.7 %all-to-all-start.2 = ((bf16[8,128,1024]{2,1,0:T(8,128)(2,1)}), bf16[8,128,1024]{2,1,0:T(8,128)(2,1)S(1)}, u32[]{:S(2)}, u32[]{:S(2)}) async-start(bf16[8,128,1024]{2,1,0:T(8,128)(2,1)} %bitcast.27), calls=%async_computation.4 | async-start | bytes 4194304 | tf_op jit(solution)/shard_map/all_to_all | solution.py:50
  125.7 32.5 %reduce-scatter.3.cloned.1.call-done = bf16[512,1024]{1,0:T(8,128)(2,1)} async-done(((bf16[2048,1024]{1,0:T(8,128)(2,1)}), bf16[512,1024]{1,0:T(8,128)(2,1)}) %reduce-scatter.3.cloned.1.call-update) | async-done | bytes 1048592 | tf_op jit(solution)/shard_map/reduce_scatter | solution.py:38
  159.8 24.1 %reduce-scatter.5.cloned.1.call-done = bf16[128,1024]{1,0:T(8,128)(2,1)} async-done(((bf16[512,1024]{1,0:T(8,128)(2,1)}), bf16[128,1024]{1,0:T(8,128)(2,1)}) %reduce-scatter.5.cloned.1.call-update) | async-done | bytes 262160 | tf_op jit(solution)/shard_map/reduce_scatter | solution.py:38
  183.9 1.2 fusion.6
  185.1 1.9 fusion.7
  (35 shorter events, 4.0 us)
Async XLA Ops:
  7.2 57.6 %all-gather.3.cloned.1.call-start = ((), (), s32[]{:S(2)}) async-start(), calls=%async_computation.5 | async-start | bytes 4456448 | tf_op jit(solution)/shard_map/all_gather | solution.py:92
  10.2 8.4 %copy-start.2 = (s32[128]{0:T(128)S(1)}, s32[128]{0:T(128)}, u32[]{:S(2)}) copy-start(s32[128]{0:T(128)} %param.7) | copy-start | bytes 1540
  14.2 31.6 %all-to-all-start = ((bf16[8,128,1024]{2,1,0:T(8,128)(2,1)}), bf16[8,128,1024]{2,1,0:T(8,128)(2,1)S(1)}, u32[]{:S(2)}, u32[]{:S(2)}) async-start(bf16[8,128,1024]{2,1,0:T(8,128)(2,1)} %broadcast_in_dim.16), calls=%async_computation | async-start | bytes 4194304 | tf_op jit(solution)/shard_map/all_to_all | solution.py:23
  76.6 19.8 %all-to-all-start.1 = ((f32[16,1,2048]{2,1,0:T(1,128)}), f32[16,1,2048]{2,1,0:T(1,128)S(1)}, u32[]{:S(2)}, u32[]{:S(2)}) async-start(f32[16,1,2048]{2,1,0:T(1,128)} %broadcast_in_dim.36), calls=%async_computation.1 | async-start | bytes 262144 | tf_op jit(solution)/shard_map/all_to_all | solution.py:23
  81.9 76.3 %reduce-scatter.3.cloned.1.call-start = ((), (), s32[]{:S(2)}) async-start(), calls=%async_computation.6 | async-start | bytes 5242880 | tf_op jit(solution)/shard_map/reduce_scatter | solution.py:38
  104.4 2.0 %copy-start.3 = (bf16[2048,1024]{1,0:T(8,128)(2,1)}, bf16[2048,1024]{1,0:T(8,128)(2,1)S(1)}, u32[]{:S(2)}) copy-start(bf16[2048,1024]{1,0:T(8,128)(2,1)S(1)} %subtract_convert_fusion) | copy-start | bytes 12582916
  121.9 36.7 %copy-start = (f32[128,1024]{1,0:T(8,128)S(1)}, f32[128,1024]{1,0:T(8,128)}, u32[]{:S(2)}) copy-start(f32[128,1024]{1,0:T(8,128)} %param.6) | copy-start | bytes 1572868
  121.9 36.3 %all-to-all-start.2 = ((bf16[8,128,1024]{2,1,0:T(8,128)(2,1)}), bf16[8,128,1024]{2,1,0:T(8,128)(2,1)S(1)}, u32[]{:S(2)}, u32[]{:S(2)}) async-start(bf16[8,128,1024]{2,1,0:T(8,128)(2,1)} %bitcast.27), calls=%async_computation.4 | async-start | bytes 4194304 | tf_op jit(solution)/shard_map/all_to_all | solution.py:50
  125.6 58.3 %copy-start.1 = (f32[128,1024]{1,0:T(8,128)S(1)}, f32[128,1024]{1,0:T(8,128)}, u32[]{:S(2)}) copy-start(f32[128,1024]{1,0:T(8,128)} %param.5) | copy-start | bytes 1572868
  125.6 58.3 %reduce-scatter.5.cloned.1.call-start = ((), (), s32[]{:S(2)}) async-start(), calls=%async_computation.7 | async-start | bytes 1310720 | tf_op jit(solution)/shard_map/reduce_scatter | solution.py:38
Sparse Core Ops, SparseCore 0:
  10.7 54.0 all-gather.2
  112.6 45.5 reduce-scatter.2
  160.6 23.2 reduce-scatter.4
where the time goes:
time: 194 us
  waiting for transfers between devices  80.6 us (42%)
  blocking collectives  36.5 us (19%)
  matrix products  34.2 us (18%)
  between operations  13.9 us (7%)
  starting transfers between devices  13.6 us (7%)
  other arithmetic  10.1 us (5%)
  local copies, waits for them, and re-layouts  4.51 us (2%)
    reduce_scatter x2, waiting for transfers between devices, summed_rows(): so_far = lax.psum_scatter(so_far, axis, scatter_dimension=0, tiled=True)  56.6 us
    all_gather x1, blocking collectives, per_device(): team_targets = lax.all_gather(positive, INNER, axis=0, tiled=True)  22.2 us
    all_gather x1, waiting for transfers between devices, per_device(): team_queries = lax.all_gather(query_round, INNER, axis=0, tiled=True)  19 us
    dot_general x5, matrix products, exponent(): lax.dot_general(query_tile_rows, column_block, (((1,), (1,)), ((), ())),...  18.8 us
    psum x1, blocking collectives, per_device(): column_total = lax.psum(column_part, 'team')  14.4 us
    all_to_all x2, starting transfers between devices, sent_to_all(): return lax.all_to_all(copies, axis, split_axis=0, concat_axis=0, tiled=True)  9.7 us
    dot_general x1, matrix products, per_device(): lax.dot_general(loss_weight, team_queries, (((0,), (0,)), ((), ())), pref...  9.41 us
    dot_general x1, matrix products, per_device(): jnp.dot(loss_weight, columns, preferred_element_type=jnp.float32)  6.06 us
  transfers between devices with their start and end apart: 6, of which 4 were waited for; matrix products, arithmetic and copies ran while one was open for 8% of the time, Pallas kernels for 0%

commit v1 on v0

v1 whole, which is shorter than its diff:
```python
import math

import jax
import jax.numpy as jnp
from jax import lax
from jax.experimental import pallas as pl
from jax.experimental.pallas import tpu as pltpu
from jax.sharding import PartitionSpec as P

MESH = pl.DeviceIdType.MESH
F32 = jnp.float32
BF16 = jnp.bfloat16

SCALE = 20.0
EXP2_SCALE = SCALE * math.log2(math.e)
EPSILON = 1e-06
RING = 4
ROWS = 128
HALF = 64
D = 1024
NQ = 2048
NP = 1024

PLACE = {
    (0, 0): 0, (0, 1): 1, (3, 0): 2, (1, 0): 3,
    (3, 1): 4, (1, 1): 5, (2, 0): 6, (2, 1): 7,
}
ORDER = sorted(PLACE, key=PLACE.get)
A, B = 0, 1
COPIES = 160


class Links:
    def __init__(self, send_sem, recv_sem):
        self.send_sem, self.recv_sem, self.copies = send_sem, recv_sem, {}

    def send(self, name, src, dst, device):
        i = len(self.copies)
        assert i < COPIES and name not in self.copies
        copy = pltpu.make_async_remote_copy(
            src_ref=src,
            dst_ref=dst,
            send_sem=self.send_sem.at[i],
            recv_sem=self.recv_sem.at[i],
            device_id=device,
            device_id_type=MESH,
        )
        copy.start()
        self.copies[name] = copy

    def arrived(self, name):
        self.copies[name].wait_recv()

    def drain(self):
        for copy in self.copies.values():
            copy.wait_send()


def kernel(
    q_hbm, p_hbm, pos_in, gq_hbm, gp_hbm,
    qf, pf, q_len, p_len, qbuf, pbuf, pos_buf, e_ref, w_ref, racc, cacc,
    row_tx, row_rx, col_tx, col_rx, row_tot, col_tot, qpart, ppart, q_d2d, q_rx, p_rx,
    local_sem, send_sem, recv_sem,
):
    team, inner = lax.axis_index("team"), lax.axis_index("inner")
    x, c = team // 2, team % 2
    z, y = inner // RING, inner % RING
    bit = y % 2

    def device(x, y, z, c):
        return {"team": x * 2 + c, "inner": z * RING + y}

    def q_device(r, s, t):
        yy = y if s == 0 else y + 1 - 2 * bit
        return device((x + r) % RING, yy, z, c if t == 0 else 1 - c)

    def p_device(r, s):
        return device(x, y if s == 0 else 3 - y, (z + r) % RING, c)

    q_peers = [(r, s, t) for r in range(RING) for s in range(2) for t in range(2)][1:]
    p_peers = [(r, s) for r in range(RING) for s in range(2)][1:]

    loads = [
        pltpu.make_async_copy(q_hbm, qf, local_sem.at[0]),
        pltpu.make_async_copy(p_hbm, pf, local_sem.at[1]),
    ]
    for load in loads:
        load.start()
    barrier = pltpu.get_barrier_semaphore()
    for peer in q_peers:
        pl.semaphore_signal(barrier, inc=1, device_id=q_device(*peer), device_id_type=MESH)
    for peer in p_peers:
        pl.semaphore_signal(barrier, inc=1, device_id=p_device(*peer), device_id_type=MESH)

    links = Links(send_sem, recv_sem)
    send, arrived = links.send, links.arrived

    def normalize(full, length_ref, rounded):
        v = full[...]
        length = jnp.sqrt(jnp.sum(v * v, axis=1, keepdims=True) + EPSILON)
        unit = v / length
        full[...] = unit
        length_ref[...] = jnp.broadcast_to(length, (ROWS, 128))
        rounded[pl.ds(0, ROWS), :] = unit.astype(BF16)

    loads[0].wait()
    normalize(qf, q_len, qbuf)
    loads[1].wait()
    normalize(pf, p_len, pbuf)
    pos_buf[0] = jnp.broadcast_to(pos_in[...], (8, 128))
    racc[...] = jnp.zeros_like(racc)
    cacc[...] = jnp.zeros_like(cacc)
    pl.semaphore_wait(barrier, len(q_peers) + len(p_peers))

    def q_at(place, half, t=0):
        return qbuf.at[pl.ds(PLACE[place] * 256 + t * ROWS + half * HALF, HALF), :]

    def p_at(place, half):
        return pbuf.at[pl.ds(PLACE[place] * ROWS + half * HALF, HALF), :]

    class Gather:
        def __init__(self, tag, at, right, left, pair, on_arrival):
            self.tag, self.at, self.on_arrival = tag, at, on_arrival
            self.to = {"x": right, "l": left, "y": pair}
            self.landed = {}

        def send(self, name, src, dst, half):
            self.landed[name] = (dst, half)
            send(self.tag + name, self.at(src, half), self.at(dst, half), self.to[name[0]])

        def take(self, name):
            arrived(self.tag + name)
            self.on_arrival(name, *self.landed[name])

        def begin(self):
            self.send("xA", (0, 0), (3, 0), A)
            self.send("lA", (0, 0), (1, 0), A)
            self.send("yB", (0, 0), (0, 1), B)
            self.send("xB", (0, 0), (3, 0), B)
            self.send("lB", (0, 0), (1, 0), B)
            self.send("yA", (0, 0), (0, 1), A)

        def first(self):
            self.take("xA")
            self.send("xA2", (3, 0), (2, 0), A)
            self.send("yA3", (3, 0), (3, 1), A)
            self.take("lA")
            self.send("yA1", (1, 0), (1, 1), A)
            self.take("yB")
            self.send("xPB", (0, 1), (3, 1), B)
            self.send("lPB", (0, 1), (1, 1), B)

        def second(self):
            self.take("xB")
            self.send("xB2", (3, 0), (2, 0), B)
            self.take("lB")
            self.take("yA")

        def third(self):
            self.take("lPB")
            self.send("lPB2", (1, 1), (2, 1), B)
            self.take("xA2")
            self.send("yA2", (2, 0), (2, 1), A)
            self.take("yA3")

        def fourth(self):
            self.take("xPB")
            self.take("yA1")

        def fifth(self):
            self.take("xB2")
            self.take("lPB2")
            self.take("yA2")

    sibling = q_device(0, 0, 1)

    def share(name, place, half):
        send("c" + name, q_at(place, half, 0), q_at(place, half, 1), sibling)

    qg = Gather("q", q_at, q_device(1, 0, 0), q_device(3, 0, 0), q_device(0, 1, 0), share)
    pg = Gather("p", p_at, p_device(1, 0), p_device(3, 0), p_device(0, 1), lambda *_: None)
    qg.begin()
    pg.begin()
    send("c", qbuf.at[pl.ds(0, ROWS), :], qbuf.at[pl.ds(ROWS, ROWS), :], sibling)
    for r, s, t in q_peers:
        slot = PLACE[(-r % RING, s)] * 2 + t
        send(f"pos{r}{s}{t}", pos_buf.at[0], pos_buf.at[slot], q_device(r, s, t))

    def scores(rows0, rows1, cols0, cols1):
        step, width = 512, 256

        @pl.loop(0, (rows1 - rows0) // step)
        def _(i):
            rows = pl.ds(pl.multiple_of(rows0 + i * step, step), step)
            for j in range(cols0, cols1, width):
                cols = pl.ds(j, width)
                s = lax.dot_general(
                    qbuf[rows, :],
                    pbuf[cols, :],
                    (((1,), (1,)), ((), ())),
                    preferred_element_type=F32,
                )
                e = jnp.exp2(s * EXP2_SCALE)
                e_ref[rows, cols] = e
                part = e[:, 0:128]
                for k in range(128, width, 128):
                    part = part + e[:, k : k + 128]
                racc[rows, :] += part
                cacc[:, cols] += jnp.sum(e.reshape(step // 8, 8, width), axis=0)

    for g in (qg, pg):
        g.first()
    for g in (qg, pg):
        g.second()
    arrived("c")
    for name in ("xA", "lA", "yB", "xB", "lB", "yA"):
        arrived("c" + name)
    scores(0, 1024, 0, 512)
    for g in (qg, pg):
        g.third()
    for g in (qg, pg):
        g.fourth()
    for name in ("lPB", "yA3", "xPB", "yA1"):
        arrived("c" + name)
    scores(0, 1024, 512, 768)
    scores(1024, 1536, 0, 768)
    for g in (qg, pg):
        g.fifth()
    scores(0, 1536, 768, 1024)
    for name in ("xA2", "xB2", "lPB2", "yA2"):
        arrived("c" + name)
    scores(1536, 2048, 0, 1024)

    def q_index(r, s, t):
        yb = bit if s == 0 else 1 - bit
        return ((x + r) % RING) * 4 + yb * 2 + (c if t == 0 else 1 - c)

    def p_index(r, s):
        yb = bit if s == 0 else 1 - bit
        return ((z + r) % RING) * 2 + yb

    for k, place in enumerate(ORDER):
        col = jnp.sum(cacc[:, pl.ds(k * ROWS, ROWS)], axis=0, keepdims=True)
        col_tx[pl.ds(p_index(*place), 1), :] = col
    for r, s in p_peers:
        send(f"col{r}{s}", col_tx, col_rx.at[(-r % RING) * 2 + s], p_device(r, s))
    for k, (place, t) in enumerate([(o, t) for o in ORDER for t in range(2)]):
        turned = jnp.transpose(racc[pl.ds(k * ROWS, ROWS), :])
        row_tx[pl.ds(q_index(*place, t), 1), :] = jnp.sum(turned, axis=0, keepdims=True)
    for r, s, t in q_peers:
        slot = (-r % RING) * 4 + s * 2 + t
        send(f"row{r}{s}{t}", row_tx, row_rx.at[slot], q_device(r, s, t))

    for peer in p_peers:
        arrived("col%d%d" % peer)
    total = col_tx[...]
    for i in range(1, 8):
        total = total + col_rx[i]
    col_inverse = 1.0 / total
    col_tot[pl.ds(0, 8), :] = col_inverse
    for peer in q_peers:
        arrived("pos%d%d%d" % peer)
    for peer in q_peers:
        arrived("row%d%d%d" % peer)
    total = row_tx[...]
    for i in range(1, 16):
        total = total + row_rx[i]
    row_tot[pl.ds(0, 16), :] = 1.0 / total
    for k, (place, t) in enumerate([(o, t) for o in ORDER for t in range(2)]):
        row_tot[pl.ds(16 + k, 1), :] = row_tot[pl.ds(q_index(*place, t), 1), :]
    for k, place in enumerate(ORDER):
        col_tot[pl.ds(8 + k, 1), :] = col_tot[pl.ds(p_index(*place), 1), :]

    def column_base(place):
        r, s = place
        zz, yy = (z + r) % RING, y if s == 0 else 3 - y
        return (team * 16 + zz * RING + yy) * ROWS

    bases = [column_base(place).astype(F32) for place in ORDER]

    def weights(first, last):
        @pl.loop(first, last)
        def _(k):
            rows = pl.ds(pl.multiple_of(k * ROWS, ROWS), ROWS)
            row_inverse = jnp.transpose(jnp.broadcast_to(row_tot[pl.ds(16 + k, 1), :], (128, 128)))
            target = jnp.transpose(
                jnp.broadcast_to(pos_buf[k, pl.ds(0, 1), :].astype(F32), (128, 128))
            )
            lane = lax.broadcasted_iota(jnp.int32, (ROWS, 128), 1).astype(F32)
            shifted = target - lane
            for j in range(8):
                cols = pl.ds(j * 128, 128)
                w = e_ref[rows, cols] * (row_inverse + col_tot[pl.ds(8 + j, 1), :])
                w = w - jnp.where(shifted == bases[j], 2.0, 0.0)
                w_ref[rows, cols] = w.astype(BF16)

    def q_dot(g):
        rows = pl.ds(g * 512, 512)
        for j in range(0, D, 256):
            cols = pl.ds(j, 256)
            qpart[rows, cols] = jnp.dot(
                w_ref[rows, :], pbuf[:, cols], preferred_element_type=F32
            ).astype(BF16)
        for k in (2 * g, 2 * g + 1):
            send(f"d{k}", qpart.at[pl.ds(k * 256 + ROWS, ROWS), :], q_d2d.at[k], sibling)

    def p_dot(g):
        out = pl.ds(g * 256, 256)
        for j in range(0, D, 256):
            cols = pl.ds(j, 256)
            ppart[out, cols] = lax.dot_general(
                w_ref[:, out],
                qbuf[:, cols],
                (((0,), (0,)), ((), ())),
                preferred_element_type=F32,
            ).astype(BF16)

    class Reduce:
        def __init__(self, tag, part, stride, extra, rx, right, left, pair):
            self.tag, self.part, self.stride, self.extra, self.rx = tag, part, stride, extra, rx
            self.to = {"x": right, "l": left, "y": pair}
            self.slots = {}

        def rows(self, place, half):
            return pl.ds(PLACE[place] * self.stride + half * HALF, HALF)

        def total(self, place, half, names):
            value = self.part[self.rows(place, half), :].astype(F32)
            if self.extra is not None:
                value += self.extra[PLACE[place], pl.ds(half * HALF, HALF), :].astype(F32)
            for name in names:
                arrived(self.tag + name)
                value += self.rx[self.slots[name]].astype(F32)
            return value

        def send(self, name, place, half, *names):
            if names or self.extra is not None:
                self.part[self.rows(place, half), :] = self.total(place, half, names).astype(BF16)
            self.slots[name] = slot = len(self.slots)
            src = self.part.at[self.rows(place, half), :]
            send(self.tag + name, src, self.rx.at[slot], self.to[name[0]])

        def one(self):
            self.send("xB0o", (2, 0), B)
            self.send("lB1o", (2, 1), B)
            self.send("yA2", (2, 1), A)

        def two(self):
            self.send("xB1r", (1, 1), B)
            self.send("yA1", (1, 1), A)
            self.send("yA3", (3, 1), A)

        def three(self):
            self.send("lB0l", (3, 0), B)
            self.send("xAo", (2, 0), A, "yA2")

        def four(self):
            self.send("yA0", (0, 1), A)
            self.send("lB1l", (3, 1), B, "lB1o")
            self.send("xB0r", (1, 0), B, "xB0o")

        def five(self):
            self.send("lAl", (3, 0), A, "yA3")
            self.send("yB1f", (0, 1), B, "xB1r", "lB1l")
            self.send("xAr", (1, 0), A, "yA1", "xAo")

        def finish(self, unit_ref, length_ref, out_ref):
            for half, names in ((B, ("xB0r", "lB0l", "yB1f")), (A, ("yA0", "lAl", "xAr"))):
                rows = pl.ds(half * HALF, HALF)
                raw = self.total((0, 0), half, names) * SCALE
                unit = unit_ref[rows, :]
                along = jnp.sum(unit * raw, axis=1, keepdims=True)
                out_ref[rows, :] = (raw - unit * along) / length_ref[rows, 0:1]

    qr = Reduce(
        "Q", qpart, 256, q_d2d, q_rx, q_device(1, 0, 0), q_device(3, 0, 0), q_device(0, 1, 0)
    )
    pr = Reduce("P", ppart, 128, None, p_rx, p_device(1, 0), p_device(3, 0), p_device(0, 1))

    def shared(*places):
        for k in places:
            arrived(f"d{k}")

    weights(12, 16)
    q_dot(3)
    weights(0, 12)
    shared(6, 7)
    qr.one()
    p_dot(3)
    pr.one()
    q_dot(2)
    p_dot(2)
    pr.two()
    shared(4, 5)
    qr.two()
    q_dot(1)
    p_dot(1)
    shared(2, 3)
    qr.three()
    pr.three()
    q_dot(0)
    p_dot(0)
    shared(0, 1)
    qr.four()
    pr.four()
    qr.five()
    pr.five()
    qr.finish(qf, q_len, qf)
    store_q = pltpu.make_async_copy(qf, gq_hbm, local_sem.at[0])
    store_q.start()
    pr.finish(pf, p_len, pf)
    store_p = pltpu.make_async_copy(pf, gp_hbm, local_sem.at[1])
    store_p.start()
    links.drain()
    store_q.wait()
    store_p.wait()


def per_device(queries, passages, positive):
    vmem = pltpu.VMEM
    anywhere = pl.BlockSpec(memory_space=pl.ANY)
    scratch = [
        vmem((ROWS, D), F32),
        vmem((ROWS, D), F32),
        vmem((ROWS, 128), F32),
        vmem((ROWS, 128), F32),
        vmem((NQ, D), BF16),
        vmem((NP, D), BF16),
        vmem((16, 8, 128), jnp.int32),
        vmem((NQ, NP), F32),
        vmem((NQ, NP), BF16),
        vmem((NQ, 128), F32),
        vmem((8, NP), F32),
        vmem((16, 128), F32),
        vmem((16, 16, 128), F32),
        vmem((8, 128), F32),
        vmem((8, 8, 128), F32),
        vmem((32, 128), F32),
        vmem((16, 128), F32),
        vmem((NQ, D), BF16),
        vmem((NP, D), BF16),
        vmem((8, ROWS, D), BF16),
        vmem((14, HALF, D), BF16),
        vmem((14, HALF, D), BF16),
        pltpu.SemaphoreType.DMA((2,)),
        pltpu.SemaphoreType.DMA((COPIES,)),
        pltpu.SemaphoreType.DMA((COPIES,)),
    ]
    out = jax.ShapeDtypeStruct((ROWS, D), F32)
    return pl.pallas_call(
        kernel,
        out_shape=(out, out),
        in_specs=[anywhere, anywhere, pl.BlockSpec(memory_space=pltpu.VMEM)],
        out_specs=(anywhere, anywhere),
        scratch_shapes=scratch,
        compiler_params=pltpu.CompilerParams(
            collective_id=0, has_side_effects=True, vmem_limit_bytes=60 << 20
        ),
    )(queries, passages, positive.reshape(1, ROWS))


def solution(mesh):
    rows = P(("team", "inner"), None)
    return jax.shard_map(
        per_device,
        mesh=mesh,
        in_specs=(rows, rows, P(("team", "inner"))),
        out_specs=(rows, rows),
        check_vma=False,
    )
```

time: 194 us -> 66.5 us (0.34)
  waiting for transfers between devices: 80.6 us -> 0 us
  Pallas kernels: 0 us -> 63 us
  blocking collectives: 36.5 us -> 0 us
  matrix products: 34.2 us -> 0 us
  starting transfers between devices: 13.6 us -> 0 us
  between operations: 13.9 us -> 0.65 us
  other arithmetic: 10.1 us -> 0 us
    pallas_call x0 -> x1, Pallas kernels: none -> 63 us  [per_device(): pl.pallas_call(kernel, out_shape=(out, out), in_specs=[anywhere, anywhere...]
    reduce_scatter x2 -> x0, waiting for transfers between devices: 56.6 us -> none  [summed_rows(): so_far = lax.psum_scatter(so_far, axis, scatter_dimension=0, tiled=True)]
    dot_general x7 -> x0, matrix products: 34.2 us -> none  [the longest x5 18.8 us: exponent(): lax.dot_general(query_tile_rows, column_block, (((1,), (1,)), ((), ())),...]
    all_gather x1 -> x0, blocking collectives: 22.2 us -> none  [per_device(): team_targets = lax.all_gather(positive, INNER, axis=0, tiled=True)]
    all_gather x1 -> x0, waiting for transfers between devices: 19 us -> none  [per_device(): team_queries = lax.all_gather(query_round, INNER, axis=0, tiled=True)]
    psum x1 -> x0, blocking collectives: 14.4 us -> none  [per_device(): column_total = lax.psum(column_part, 'team')]
    all_to_all x3 -> x0, starting transfers between devices: 13.4 us -> none  [the longest x2 9.7 us: sent_to_all(): return lax.all_to_all(copies, axis, split_axis=0, concat_axis=0, tiled=True)]
    all_to_all x3 -> x0, waiting for transfers between devices: 5 us -> none  [the longest x2 5 us: sent_to_all(): return lax.all_to_all(copies, axis, split_axis=0, concat_axis=0, tiled=True)]
  transfers between devices with their start and end apart: 6 -> 0, of which waited for: 4 -> 0; matrix products, arithmetic and copies ran while one was open for 8% -> 0% of each run, Pallas kernels for 0% -> 0%
where the time goes in v1:
time: 66.5 us; the launch traced here: 66.4 us
  Pallas kernels  63 us (95%)
  local copies, waits for them, and re-layouts  2.74 us (4%)
    pallas_call x1, Pallas kernels, per_device(): pl.pallas_call(kernel, out_shape=(out, out), in_specs=[anywhere, anywhere...  63 us
    unnamed x4, local copies, waits for them, and re-layouts  2.74 us

profile of v1, /device:TPU:0, one launch (start us, length us, event | category | flops | bytes accessed | tf_op | source)
XLA Modules:
  0.0 66.4 jit_solution(1568846764443282219)
XLA Ops:
  0.6 63.0 %shard_map.50 = (f32[128,1024]{1,0:T(8,128)}, f32[128,1024]{1,0:T(8,128)}) custom-call(f32[128,1024]{1,0:T(8,128)} %q_hbm.1, f32[128,1024]{1,0:T(8,128)} %p_hbm.1, s32[1,128]{1,0:T(1,128)} %bitcast.1), custom_call_target="tpu_custom_call" | custom-call | tf_op jit(solution)/shard_map/pallas_call | solution.py:450
  63.6 0.0 copy-start
  63.6 1.9 %copy.7 = f32[128,1024]{1,0:T(8,128)} copy(f32[128,1024]{1,0:T(8,128)} %get-tuple-element.4) | data formatting | bytes 1048576
  65.6 0.0 copy-done
  65.6 0.8 %copy.8 = f32[128,1024]{1,0:T(8,128)} copy(f32[128,1024]{1,0:T(8,128)S(1)} %copy-done) | data formatting | bytes 1048576
Async XLA Ops:
  63.6 2.0 %copy-start = (f32[128,1024]{1,0:T(8,128)S(1)}, f32[128,1024]{1,0:T(8,128)}, u32[]{:S(2)}) copy-start(f32[128,1024]{1,0:T(8,128)} %get-tuple-element.5) | copy-start | bytes 1572868

commit v2 on v1

--- a/solution.py
+++ b/solution.py
@@ -27,40 +27,55 @@
 }
 ORDER = sorted(PLACE, key=PLACE.get)
 A, B = 0, 1
-COPIES = 160
+SEMAPHORES = 75
+
+
+def q_row(place, t):
+    k = PLACE[place]
+    return t * 512 + k * ROWS if k < 4 else k // 2 * 512 + t * 256 + k % 2 * ROWS
 
 
 class Links:
-    def __init__(self, send_sem, recv_sem):
-        self.send_sem, self.recv_sem, self.copies = send_sem, recv_sem, {}
-
-    def send(self, name, src, dst, device):
-        i = len(self.copies)
-        assert i < COPIES and name not in self.copies
-        copy = pltpu.make_async_remote_copy(
+    def __init__(self, semaphores, device):
+        self.semaphores, self.device = semaphores, device
+        self.index, self.copies = {}, {}
+
+    def semaphore(self, name):
+        i = self.index.setdefault(name, len(self.index))
+        assert i < SEMAPHORES
+        return self.semaphores.at[i]
+
+    def copy(self, src, dst, sent, landed, device):
+        return pltpu.make_async_remote_copy(
             src_ref=src,
             dst_ref=dst,
-            send_sem=self.send_sem.at[i],
-            recv_sem=self.recv_sem.at[i],
+            send_sem=self.semaphore("sent " + sent),
+            recv_sem=self.semaphore("landed " + landed),
             device_id=device,
             device_id_type=MESH,
         )
+
+    def send(self, name, src, dst, device, sent, landed=None):
+        copy = self.copy(src, dst, sent, landed or name, device)
         copy.start()
+        assert name not in self.copies
         self.copies[name] = copy
 
     def arrived(self, name):
         self.copies[name].wait_recv()
 
-    def drain(self):
-        for copy in self.copies.values():
-            copy.wait_send()
+    def all_arrived(self, landed, like):
+        self.copy(like, like, "c", landed, self.device).wait_recv()
+
+    def all_sent(self, sent, like):
+        self.copy(like, like, sent, "c1", self.device).wait_send()
 
 
 def kernel(
-    q_hbm, p_hbm, pos_in, gq_hbm, gp_hbm,
+    q_hbm, p_hbm, pos_in, q_out, p_out,
     qf, pf, q_len, p_len, qbuf, pbuf, pos_buf, e_ref, w_ref, racc, cacc,
     row_tx, row_rx, col_tx, col_rx, row_tot, col_tot, qpart, ppart, q_d2d, q_rx, p_rx,
-    local_sem, send_sem, recv_sem,
+    local_sem, copy_sem,
 ):
     team, inner = lax.axis_index("team"), lax.axis_index("inner")
     x, c = team // 2, team % 2
@@ -87,12 +102,13 @@
     for load in loads:
         load.start()
     barrier = pltpu.get_barrier_semaphore()
-    for peer in q_peers:
-        pl.semaphore_signal(barrier, inc=1, device_id=q_device(*peer), device_id_type=MESH)
-    for peer in p_peers:
-        pl.semaphore_signal(barrier, inc=1, device_id=p_device(*peer), device_id_type=MESH)
-
-    links = Links(send_sem, recv_sem)
+    neighbours = [q_device(*peer) for peer in ((1, 0, 0), (3, 0, 0), (0, 1, 0), (0, 0, 1))]
+    neighbours += [p_device(*peer) for peer in ((1, 0), (3, 0), (0, 1))]
+    for neighbour in neighbours:
+        pl.semaphore_signal(barrier, inc=1, device_id=neighbour, device_id_type=MESH)
+
+    sibling = q_device(0, 0, 1)
+    links = Links(copy_sem, sibling)
     send, arrived = links.send, links.arrived
 
     def normalize(full, length_ref, rounded):
@@ -110,10 +126,10 @@
     pos_buf[0] = jnp.broadcast_to(pos_in[...], (8, 128))
     racc[...] = jnp.zeros_like(racc)
     cacc[...] = jnp.zeros_like(cacc)
-    pl.semaphore_wait(barrier, len(q_peers) + len(p_peers))
+    pl.semaphore_wait(barrier, len(neighbours))
 
     def q_at(place, half, t=0):
-        return qbuf.at[pl.ds(PLACE[place] * 256 + t * ROWS + half * HALF, HALF), :]
+        return qbuf.at[pl.ds(q_row(place, t) + half * HALF, HALF), :]
 
     def p_at(place, half):
         return pbuf.at[pl.ds(PLACE[place] * ROWS + half * HALF, HALF), :]
@@ -126,7 +142,7 @@
 
         def send(self, name, src, dst, half):
             self.landed[name] = (dst, half)
-            send(self.tag + name, self.at(src, half), self.at(dst, half), self.to[name[0]])
+            send(self.tag + name, self.at(src, half), self.at(dst, half), self.to[name[0]], self.tag)
 
         def take(self, name):
             arrived(self.tag + name)
@@ -172,22 +188,18 @@
             self.take("lPB2")
             self.take("yA2")
 
-    sibling = q_device(0, 0, 1)
-
     def share(name, place, half):
-        send("c" + name, q_at(place, half, 0), q_at(place, half, 1), sibling)
+        stage = "c1" if PLACE[place] < 4 else "c2" if PLACE[place] < 6 else "c3"
+        send("c" + name, q_at(place, half, 0), q_at(place, half, 1), sibling, "c", stage)
 
     qg = Gather("q", q_at, q_device(1, 0, 0), q_device(3, 0, 0), q_device(0, 1, 0), share)
     pg = Gather("p", p_at, p_device(1, 0), p_device(3, 0), p_device(0, 1), lambda *_: None)
     qg.begin()
     pg.begin()
-    send("c", qbuf.at[pl.ds(0, ROWS), :], qbuf.at[pl.ds(ROWS, ROWS), :], sibling)
-    for r, s, t in q_peers:
-        slot = PLACE[(-r % RING, s)] * 2 + t
-        send(f"pos{r}{s}{t}", pos_buf.at[0], pos_buf.at[slot], q_device(r, s, t))
-
-    def scores(rows0, rows1, cols0, cols1):
-        step, width = 512, 256
+    send("c", qbuf.at[pl.ds(0, ROWS), :], qbuf.at[pl.ds(512, ROWS), :], sibling, "c", "c1")
+
+    def scores(rows0, rows1, cols0, cols1, step=512):
+        width = 256
 
         @pl.loop(0, (rows1 - rows0) // step)
         def _(i):
@@ -208,28 +220,34 @@
                 racc[rows, :] += part
                 cacc[:, cols] += jnp.sum(e.reshape(step // 8, 8, width), axis=0)
 
+    def landed(stage, rows, count):
+        links.all_arrived(stage, qbuf.at[pl.ds(rows, count), :])
+
     for g in (qg, pg):
         g.first()
     for g in (qg, pg):
         g.second()
-    arrived("c")
-    for name in ("xA", "lA", "yB", "xB", "lB", "yA"):
-        arrived("c" + name)
-    scores(0, 1024, 0, 512)
+    scores(0, 512, 0, 512)
+    landed("c1", 512, 512)
+    scores(512, 1024, 0, 512)
     for g in (qg, pg):
         g.third()
     for g in (qg, pg):
         g.fourth()
-    for name in ("lPB", "yA3", "xPB", "yA1"):
-        arrived("c" + name)
     scores(0, 1024, 512, 768)
-    scores(1024, 1536, 0, 768)
+    scores(1024, 1280, 0, 768, 256)
+    landed("c2", 1280, 256)
+    scores(1280, 1536, 0, 768, 256)
     for g in (qg, pg):
         g.fifth()
+    blocks = [(place, t) for place in ORDER for t in range(2)]
+    for r, s, t in q_peers:
+        slot = q_row((-r % RING, s), t) // ROWS
+        send(f"pos{r}{s}{t}", pos_buf.at[0], pos_buf.at[slot], q_device(r, s, t), "pos", "pos")
     scores(0, 1536, 768, 1024)
-    for name in ("xA2", "xB2", "lPB2", "yA2"):
-        arrived("c" + name)
-    scores(1536, 2048, 0, 1024)
+    scores(1536, 1792, 0, 1024, 256)
+    landed("c3", 1792, 256)
+    scores(1792, 2048, 0, 1024, 256)
 
     def q_index(r, s, t):
         yb = bit if s == 0 else 1 - bit
@@ -243,31 +261,29 @@
         col = jnp.sum(cacc[:, pl.ds(k * ROWS, ROWS)], axis=0, keepdims=True)
         col_tx[pl.ds(p_index(*place), 1), :] = col
     for r, s in p_peers:
-        send(f"col{r}{s}", col_tx, col_rx.at[(-r % RING) * 2 + s], p_device(r, s))
-    for k, (place, t) in enumerate([(o, t) for o in ORDER for t in range(2)]):
-        turned = jnp.transpose(racc[pl.ds(k * ROWS, ROWS), :])
+        slot = (-r % RING) * 2 + s
+        send(f"col{r}{s}", col_tx, col_rx.at[slot], p_device(r, s), "col", "col")
+    for place, t in blocks:
+        turned = jnp.transpose(racc[pl.ds(q_row(place, t), ROWS), :])
         row_tx[pl.ds(q_index(*place, t), 1), :] = jnp.sum(turned, axis=0, keepdims=True)
     for r, s, t in q_peers:
         slot = (-r % RING) * 4 + s * 2 + t
-        send(f"row{r}{s}{t}", row_tx, row_rx.at[slot], q_device(r, s, t))
-
-    for peer in p_peers:
-        arrived("col%d%d" % peer)
+        send(f"row{r}{s}{t}", row_tx, row_rx.at[slot], q_device(r, s, t), "row", "row")
+
+    links.all_arrived("col", col_rx.at[pl.ds(1, 7)])
     total = col_tx[...]
     for i in range(1, 8):
         total = total + col_rx[i]
     col_inverse = 1.0 / total
     col_tot[pl.ds(0, 8), :] = col_inverse
-    for peer in q_peers:
-        arrived("pos%d%d%d" % peer)
-    for peer in q_peers:
-        arrived("row%d%d%d" % peer)
+    links.all_arrived("pos", pos_buf.at[pl.ds(1, 15)])
+    links.all_arrived("row", row_rx.at[pl.ds(1, 15)])
     total = row_tx[...]
     for i in range(1, 16):
         total = total + row_rx[i]
     row_tot[pl.ds(0, 16), :] = 1.0 / total
-    for k, (place, t) in enumerate([(o, t) for o in ORDER for t in range(2)]):
-        row_tot[pl.ds(16 + k, 1), :] = row_tot[pl.ds(q_index(*place, t), 1), :]
+    for place, t in blocks:
+        row_tot[pl.ds(16 + q_row(place, t) // ROWS, 1), :] = row_tot[pl.ds(q_index(*place, t), 1), :]
     for k, place in enumerate(ORDER):
         col_tot[pl.ds(8 + k, 1), :] = col_tot[pl.ds(p_index(*place), 1), :]
 
@@ -278,7 +294,7 @@
 
     bases = [column_base(place).astype(F32) for place in ORDER]
 
-    def weights(first, last):
+    def weights(first, last, cols0, cols1):
         @pl.loop(first, last)
         def _(k):
             rows = pl.ds(pl.multiple_of(k * ROWS, ROWS), ROWS)
@@ -288,24 +304,34 @@
             )
             lane = lax.broadcasted_iota(jnp.int32, (ROWS, 128), 1).astype(F32)
             shifted = target - lane
-            for j in range(8):
+            for j in range(cols0, cols1):
                 cols = pl.ds(j * 128, 128)
                 w = e_ref[rows, cols] * (row_inverse + col_tot[pl.ds(8 + j, 1), :])
                 w = w - jnp.where(shifted == bases[j], 2.0, 0.0)
                 w_ref[rows, cols] = w.astype(BF16)
 
-    def q_dot(g):
-        rows = pl.ds(g * 512, 512)
+    def q_dot(first, last):
+        rows = pl.ds(first, last - first)
         for j in range(0, D, 256):
             cols = pl.ds(j, 256)
             qpart[rows, cols] = jnp.dot(
                 w_ref[rows, :], pbuf[:, cols], preferred_element_type=F32
             ).astype(BF16)
-        for k in (2 * g, 2 * g + 1):
-            send(f"d{k}", qpart.at[pl.ds(k * 256 + ROWS, ROWS), :], q_d2d.at[k], sibling)
-
-    def p_dot(g):
-        out = pl.ds(g * 256, 256)
+
+    def q_dots(own, other, blocks, shared_first):
+        q_dot(other, other + blocks * ROWS)
+        rows = blocks * ROWS
+        send(
+            f"d{shared_first}",
+            qpart.at[pl.ds(other, rows), :],
+            q_d2d.at[pl.ds(shared_first, rows), :],
+            sibling,
+            "d",
+        )
+        q_dot(own, own + rows)
+
+    def p_dot(first, last):
+        out = pl.ds(first, last - first)
         for j in range(0, D, 256):
             cols = pl.ds(j, 256)
             ppart[out, cols] = lax.dot_general(
@@ -316,18 +342,19 @@
             ).astype(BF16)
 
     class Reduce:
-        def __init__(self, tag, part, stride, extra, rx, right, left, pair):
-            self.tag, self.part, self.stride, self.extra, self.rx = tag, part, stride, extra, rx
+        def __init__(self, tag, part, row, extra, rx, right, left, pair):
+            self.tag, self.part, self.row, self.extra, self.rx = tag, part, row, extra, rx
             self.to = {"x": right, "l": left, "y": pair}
             self.slots = {}
 
         def rows(self, place, half):
-            return pl.ds(PLACE[place] * self.stride + half * HALF, HALF)
+            return pl.ds(self.row(place) + half * HALF, HALF)
 
         def total(self, place, half, names):
             value = self.part[self.rows(place, half), :].astype(F32)
             if self.extra is not None:
-                value += self.extra[PLACE[place], pl.ds(half * HALF, HALF), :].astype(F32)
+                rows = pl.ds(PLACE[place] * ROWS + half * HALF, HALF)
+                value += self.extra[rows, :].astype(F32)
             for name in names:
                 arrived(self.tag + name)
                 value += self.rx[self.slots[name]].astype(F32)
@@ -338,7 +365,7 @@
                 self.part[self.rows(place, half), :] = self.total(place, half, names).astype(BF16)
             self.slots[name] = slot = len(self.slots)
             src = self.part.at[self.rows(place, half), :]
-            send(self.tag + name, src, self.rx.at[slot], self.to[name[0]])
+            send(self.tag + name, src, self.rx.at[slot], self.to[name[0]], self.tag)
 
         def one(self):
             self.send("xB0o", (2, 0), B)
@@ -351,17 +378,19 @@
             self.send("yA3", (3, 1), A)
 
         def three(self):
+            self.send("lB1l", (3, 1), B, "lB1o")
+            self.send("xAo", (2, 0), A, "yA2")
+
+        def four(self):
             self.send("lB0l", (3, 0), B)
-            self.send("xAo", (2, 0), A, "yA2")
-
-        def four(self):
+            self.send("xB0r", (1, 0), B, "xB0o")
             self.send("yA0", (0, 1), A)
-            self.send("lB1l", (3, 1), B, "lB1o")
-            self.send("xB0r", (1, 0), B, "xB0o")
 
         def five(self):
+            self.send("yB1f", (0, 1), B, "xB1r", "lB1l")
+
+        def six(self):
             self.send("lAl", (3, 0), A, "yA3")
-            self.send("yB1f", (0, 1), B, "xB1r", "lB1l")
             self.send("xAr", (1, 0), A, "yA1", "xAo")
 
         def finish(self, unit_ref, length_ref, out_ref):
@@ -373,52 +402,68 @@
                 out_ref[rows, :] = (raw - unit * along) / length_ref[rows, 0:1]
 
     qr = Reduce(
-        "Q", qpart, 256, q_d2d, q_rx, q_device(1, 0, 0), q_device(3, 0, 0), q_device(0, 1, 0)
+        "Q", qpart, lambda place: q_row(place, 0), q_d2d, q_rx,
+        q_device(1, 0, 0), q_device(3, 0, 0), q_device(0, 1, 0),
     )
-    pr = Reduce("P", ppart, 128, None, p_rx, p_device(1, 0), p_device(3, 0), p_device(0, 1))
-
-    def shared(*places):
-        for k in places:
-            arrived(f"d{k}")
-
-    weights(12, 16)
-    q_dot(3)
-    weights(0, 12)
-    shared(6, 7)
+    pr = Reduce(
+        "P", ppart, lambda place: PLACE[place] * ROWS, None, p_rx,
+        p_device(1, 0), p_device(3, 0), p_device(0, 1),
+    )
+
+    weights(12, 16, 0, 8)
+    q_dots(1536, 1792, 2, 768)
+    weights(0, 12, 6, 8)
+    arrived("d768")
     qr.one()
-    p_dot(3)
+    p_dot(768, 1024)
     pr.one()
-    q_dot(2)
-    p_dot(2)
+    weights(8, 12, 0, 6)
+    q_dots(1024, 1280, 2, 512)
+    weights(0, 8, 4, 6)
+    arrived("d512")
+    qr.two()
+    p_dot(512, 768)
     pr.two()
-    shared(4, 5)
-    qr.two()
-    q_dot(1)
-    p_dot(1)
-    shared(2, 3)
     qr.three()
+    weights(0, 8, 0, 4)
+    q_dots(128, 640, 3, 128)
     pr.three()
-    q_dot(0)
-    p_dot(0)
-    shared(0, 1)
+    arrived("d128")
     qr.four()
+    p_dot(128, 512)
     pr.four()
     qr.five()
+    q_dots(0, 512, 1, 0)
+    qr.six()
+    p_dot(0, 128)
     pr.five()
-    qr.finish(qf, q_len, qf)
-    store_q = pltpu.make_async_copy(qf, gq_hbm, local_sem.at[0])
-    store_q.start()
-    pr.finish(pf, p_len, pf)
-    store_p = pltpu.make_async_copy(pf, gp_hbm, local_sem.at[1])
-    store_p.start()
-    links.drain()
-    store_q.wait()
-    store_p.wait()
+    pr.six()
+    arrived("d0")
+    qr.finish(qf, q_len, q_out)
+    pr.finish(pf, p_len, p_out)
+    for sent, like in (
+        ("q", q_rx), ("p", p_rx), ("Q", q_rx), ("P", p_rx),
+        ("c", q_d2d), ("d", q_d2d),
+        ("pos", pos_buf.at[pl.ds(1, 15)]),
+        ("row", row_rx.at[pl.ds(1, 15)]),
+        ("col", col_rx.at[pl.ds(1, 7)]),
+    ):
+        links.all_sent(sent, like)
+
+
+def put_out(q_in, p_in, q_hbm, p_hbm, sem):
+    copies = [
+        pltpu.make_async_copy(q_in, q_hbm, sem.at[0]),
+        pltpu.make_async_copy(p_in, p_hbm, sem.at[1]),
+    ]
+    for copy in copies:
+        copy.start()
+    for copy in copies:
+        copy.wait()
 
 
 def per_device(queries, passages, positive):
     vmem = pltpu.VMEM
-    anywhere = pl.BlockSpec(memory_space=pl.ANY)
     scratch = [
         vmem((ROWS, D), F32),
         vmem((ROWS, D), F32),
@@ -439,24 +484,33 @@
         vmem((16, 128), F32),
         vmem((NQ, D), BF16),
         vmem((NP, D), BF16),
-        vmem((8, ROWS, D), BF16),
+        vmem((1024, D), BF16),
         vmem((14, HALF, D), BF16),
         vmem((14, HALF, D), BF16),
         pltpu.SemaphoreType.DMA((2,)),
-        pltpu.SemaphoreType.DMA((COPIES,)),
-        pltpu.SemaphoreType.DMA((COPIES,)),
+        pltpu.SemaphoreType.DMA((SEMAPHORES,)),
     ]
     out = jax.ShapeDtypeStruct((ROWS, D), F32)
-    return pl.pallas_call(
+    here = pl.BlockSpec(memory_space=pltpu.VMEM)
+    hbm = pl.BlockSpec(memory_space=pltpu.HBM)
+    grads = pl.pallas_call(
         kernel,
         out_shape=(out, out),
-        in_specs=[anywhere, anywhere, pl.BlockSpec(memory_space=pltpu.VMEM)],
-        out_specs=(anywhere, anywhere),
+        in_specs=[hbm, hbm, here],
+        out_specs=(here, here),
         scratch_shapes=scratch,
         compiler_params=pltpu.CompilerParams(
-            collective_id=0, has_side_effects=True, vmem_limit_bytes=60 << 20
+            collective_id=0, has_side_effects=True, vmem_limit_bytes=56 << 20
         ),
     )(queries, passages, positive.reshape(1, ROWS))
+    return pl.pallas_call(
+        put_out,
+        out_shape=(out, out),
+        in_specs=[here, here],
+        out_specs=(hbm, hbm),
+        scratch_shapes=[pltpu.SemaphoreType.DMA((2,))],
+        compiler_params=pltpu.CompilerParams(vmem_limit_bytes=1 << 20),
+    )(*grads)
 
 
 def solution(mesh):

time: 66.5 us -> 62.7 us (0.943)
  Pallas kernels: 63 us -> 59.1 us
    pallas_call x1 -> x2, Pallas kernels: 63 us -> 59.1 us  [the longest x1 58.1 us: per_device(): pl.pallas_call(kernel, out_shape=(out, out), in_specs=[hbm, hbm, here], o...]
where the time goes in v2:
time: 62.7 us; the launch traced here: 62 us
  Pallas kernels  59.1 us (94%)
  local copies, waits for them, and re-layouts  2.08 us (3%)
  between operations  0.81 us (1%)
    pallas_call x1, Pallas kernels, per_device(): pl.pallas_call(kernel, out_shape=(out, out), in_specs=[hbm, hbm, here], o...  58.1 us
    unnamed x4, local copies, waits for them, and re-layouts  2.08 us

profile of v2, /device:TPU:0, one launch (start us, length us, event | category | flops | bytes accessed | tf_op | source)
XLA Modules:
  0.0 62.0 jit_solution(15429013869922283039)
XLA Ops:
  0.6 58.1 %shard_map.50 = (f32[128,1024]{1,0:T(8,128)}, f32[128,1024]{1,0:T(8,128)}) custom-call(f32[128,1024]{1,0:T(8,128)} %q_hbm.1, f32[128,1024]{1,0:T(8,128)} %p_hbm.1, s32[1,128]{1,0:T(1,128)} %bitcast.1), custom_call_target="tpu_custom_call" | custom-call | tf_op jit(solution)/shard_map/pallas_call | solution.py:496
  58.7 0.0 copy-start
  58.7 1.0 %copy-done = f32[128,1024]{1,0:T(8,128)S(1)} copy-done((f32[128,1024]{1,0:T(8,128)S(1)}, f32[128,1024]{1,0:T(8,128)}, u32[]{:S(2)}) %copy-start) | copy-done | bytes 524312
  59.8 0.0 copy-start.1
  59.8 1.0 %copy-done.1 = f32[128,1024]{1,0:T(8,128)S(1)} copy-done((f32[128,1024]{1,0:T(8,128)S(1)}, f32[128,1024]{1,0:T(8,128)}, u32[]{:S(2)}) %copy-start.1) | copy-done | bytes 524312
  60.8 1.0 %shard_map.51 = (f32[128,1024]{1,0:T(8,128)}, f32[128,1024]{1,0:T(8,128)}) custom-call(f32[128,1024]{1,0:T(8,128)S(1)} %copy-done, f32[128,1024]{1,0:T(8,128)S(1)} %copy-done.1), custom_call_target="tpu_custom_call" | custom-call | tf_op jit(solution)/shard_map/pallas_call | solution.py:506
Async XLA Ops:
  58.7 1.0 %copy-start = (f32[128,1024]{1,0:T(8,128)S(1)}, f32[128,1024]{1,0:T(8,128)}, u32[]{:S(2)}) copy-start(f32[128,1024]{1,0:T(8,128)} %get-tuple-element.4.q_in) | copy-start | bytes 1572868
  59.8 1.0 %copy-start.1 = (f32[128,1024]{1,0:T(8,128)S(1)}, f32[128,1024]{1,0:T(8,128)}, u32[]{:S(2)}) copy-start(f32[128,1024]{1,0:T(8,128)} %get-tuple-element.5.p_in) | copy-start | bytes 1572868

commit v3 on v2

--- a/solution.py
+++ b/solution.py
@@ -75,7 +75,7 @@
     q_hbm, p_hbm, pos_in, q_out, p_out,
     qf, pf, q_len, p_len, qbuf, pbuf, pos_buf, e_ref, w_ref, racc, cacc,
     row_tx, row_rx, col_tx, col_rx, row_tot, col_tot, qpart, ppart, q_d2d, q_rx, p_rx,
-    local_sem, copy_sem,
+    shifted, row_inverse, local_sem, copy_sem,
 ):
     team, inner = lax.axis_index("team"), lax.axis_index("inner")
     x, c = team // 2, team % 2
@@ -200,10 +200,8 @@
 
     def scores(rows0, rows1, cols0, cols1, step=512):
         width = 256
-
-        @pl.loop(0, (rows1 - rows0) // step)
-        def _(i):
-            rows = pl.ds(pl.multiple_of(rows0 + i * step, step), step)
+        for i in range(rows0, rows1, step):
+            rows = pl.ds(i, step)
             for j in range(cols0, cols1, width):
                 cols = pl.ds(j, width)
                 s = lax.dot_general(
@@ -270,13 +268,17 @@
         slot = (-r % RING) * 4 + s * 2 + t
         send(f"row{r}{s}{t}", row_tx, row_rx.at[slot], q_device(r, s, t), "row", "row")
 
+    links.all_arrived("pos", pos_buf.at[pl.ds(1, 15)])
+    lane = lax.broadcasted_iota(jnp.int32, (ROWS, 128), 1).astype(F32)
+    for k in range(16):
+        target = jnp.broadcast_to(pos_buf[k, pl.ds(0, 1), :].astype(F32), (128, 128))
+        shifted[pl.ds(k * ROWS, ROWS), :] = jnp.transpose(target) - lane
     links.all_arrived("col", col_rx.at[pl.ds(1, 7)])
     total = col_tx[...]
     for i in range(1, 8):
         total = total + col_rx[i]
     col_inverse = 1.0 / total
     col_tot[pl.ds(0, 8), :] = col_inverse
-    links.all_arrived("pos", pos_buf.at[pl.ds(1, 15)])
     links.all_arrived("row", row_rx.at[pl.ds(1, 15)])
     total = row_tx[...]
     for i in range(1, 16):
@@ -294,33 +296,37 @@
 
     bases = [column_base(place).astype(F32) for place in ORDER]
 
-    def weights(first, last, cols0, cols1):
-        @pl.loop(first, last)
-        def _(k):
-            rows = pl.ds(pl.multiple_of(k * ROWS, ROWS), ROWS)
-            row_inverse = jnp.transpose(jnp.broadcast_to(row_tot[pl.ds(16 + k, 1), :], (128, 128)))
-            target = jnp.transpose(
-                jnp.broadcast_to(pos_buf[k, pl.ds(0, 1), :].astype(F32), (128, 128))
-            )
-            lane = lax.broadcasted_iota(jnp.int32, (ROWS, 128), 1).astype(F32)
-            shifted = target - lane
-            for j in range(cols0, cols1):
-                cols = pl.ds(j * 128, 128)
-                w = e_ref[rows, cols] * (row_inverse + col_tot[pl.ds(8 + j, 1), :])
-                w = w - jnp.where(shifted == bases[j], 2.0, 0.0)
-                w_ref[rows, cols] = w.astype(BF16)
-
-    def q_dot(first, last):
+    def row_factor(k):
+        rows = pl.ds(k * ROWS, ROWS)
+        factor = jnp.broadcast_to(row_tot[pl.ds(16 + k, 1), :], (128, 128))
+        row_inverse[rows, :] = jnp.transpose(factor)
+
+    def weight(k, j):
+        rows, cols = pl.ds(k * ROWS, ROWS), pl.ds(j * 128, 128)
+        w = e_ref[rows, cols] * (row_inverse[rows, :] + col_tot[pl.ds(8 + j, 1), :])
+        w = w - jnp.where(shifted[rows, :] == bases[j], 2.0, 0.0)
+        w_ref[rows, cols] = w.astype(BF16)
+
+    def weights(slots, cols):
+        return [(weight, k, j) for k in slots for j in cols]
+
+    def run(work):
+        for f, *args in work:
+            f(*args)
+
+    def q_dot(first, last, beside=()):
         rows = pl.ds(first, last - first)
-        for j in range(0, D, 256):
-            cols = pl.ds(j, 256)
+        for i in range(4):
+            cols = pl.ds(i * 256, 256)
             qpart[rows, cols] = jnp.dot(
                 w_ref[rows, :], pbuf[:, cols], preferred_element_type=F32
             ).astype(BF16)
-
-    def q_dots(own, other, blocks, shared_first):
-        q_dot(other, other + blocks * ROWS)
+            run(beside[len(beside) * i // 4 : len(beside) * (i + 1) // 4])
+
+    def q_dots(own, other, blocks, shared_first, beside=()):
+        half = len(beside) // 2
         rows = blocks * ROWS
+        q_dot(other, other + rows, beside[:half])
         send(
             f"d{shared_first}",
             qpart.at[pl.ds(other, rows), :],
@@ -328,18 +334,19 @@
             sibling,
             "d",
         )
-        q_dot(own, own + rows)
-
-    def p_dot(first, last):
+        q_dot(own, own + rows, beside[half:])
+
+    def p_dot(first, last, tiles=range(4), beside=()):
         out = pl.ds(first, last - first)
-        for j in range(0, D, 256):
-            cols = pl.ds(j, 256)
+        for n, i in enumerate(tiles):
+            cols = pl.ds(i * 256, 256)
             ppart[out, cols] = lax.dot_general(
                 w_ref[:, out],
                 qbuf[:, cols],
                 (((0,), (0,)), ((), ())),
                 preferred_element_type=F32,
             ).astype(BF16)
+            run(beside[len(beside) * n // len(tiles) : len(beside) * (n + 1) // len(tiles)])
 
     class Reduce:
         def __init__(self, tag, part, row, extra, rx, right, left, pair):
@@ -410,27 +417,31 @@
         p_device(1, 0), p_device(3, 0), p_device(0, 1),
     )
 
-    weights(12, 16, 0, 8)
-    q_dots(1536, 1792, 2, 768)
-    weights(0, 12, 6, 8)
+    for k in range(12, 16):
+        row_factor(k)
+    run(weights(range(12, 16), range(8)))
+    later = [(row_factor, k) for k in range(12)] + weights(range(12), (6, 7))
+    q_dots(1536, 1792, 2, 768, later)
+    later = weights(range(8, 12), range(6))
+    p_dot(768, 1024, (0, 1), later[:12])
     arrived("d768")
     qr.one()
-    p_dot(768, 1024)
+    p_dot(768, 1024, (2, 3), later[12:])
     pr.one()
-    weights(8, 12, 0, 6)
-    q_dots(1024, 1280, 2, 512)
-    weights(0, 8, 4, 6)
+    q_dots(1024, 1280, 2, 512, weights(range(8), (4, 5)))
+    later = weights(range(8), range(4))
+    p_dot(512, 768, (0, 1), later[:16])
     arrived("d512")
     qr.two()
-    p_dot(512, 768)
+    p_dot(512, 768, (2, 3), later[16:])
     pr.two()
     qr.three()
-    weights(0, 8, 0, 4)
     q_dots(128, 640, 3, 128)
     pr.three()
+    p_dot(128, 512, (0, 1))
     arrived("d128")
     qr.four()
-    p_dot(128, 512)
+    p_dot(128, 512, (2, 3))
     pr.four()
     qr.five()
     q_dots(0, 512, 1, 0)
@@ -487,6 +498,8 @@
         vmem((1024, D), BF16),
         vmem((14, HALF, D), BF16),
         vmem((14, HALF, D), BF16),
+        vmem((NQ, 128), F32),
+        vmem((NQ, 128), F32),
         pltpu.SemaphoreType.DMA((2,)),
         pltpu.SemaphoreType.DMA((SEMAPHORES,)),
     ]
@@ -500,7 +513,7 @@
         out_specs=(here, here),
         scratch_shapes=scratch,
         compiler_params=pltpu.CompilerParams(
-            collective_id=0, has_side_effects=True, vmem_limit_bytes=56 << 20
+            collective_id=0, has_side_effects=True, vmem_limit_bytes=52 << 20
         ),
     )(queries, passages, positive.reshape(1, ROWS))
     return pl.pallas_call(

time: 62.7 us -> 56.6 us (0.903)
  Pallas kernels: 59.1 us -> 53.5 us
    pallas_call x1, Pallas kernels: 58.1 us -> 52.5 us  [per_device(): pl.pallas_call(kernel, out_shape=(out, out), in_specs=[hbm, hbm, here], o...]
where the time goes in v3:
time: 56.6 us; the launch traced here: 56 us
  Pallas kernels  53.5 us (95%)
  local copies, waits for them, and re-layouts  1.69 us (3%)
  between operations  0.81 us (1%)
    pallas_call x1, Pallas kernels, per_device(): pl.pallas_call(kernel, out_shape=(out, out), in_specs=[hbm, hbm, here], o...  52.5 us
    unnamed x4, local copies, waits for them, and re-layouts  1.69 us

profile of v3, /device:TPU:0, one launch (start us, length us, event | category | flops | bytes accessed | tf_op | source)
XLA Modules:
  0.0 56.0 jit_solution(8699693034279101414)
XLA Ops:
  0.6 0.0 copy-start.1
  0.6 0.6 %copy-done.1 = s32[128]{0:T(128)S(1)} copy-done((s32[128]{0:T(128)S(1)}, s32[128]{0:T(128)}, u32[]{:S(2)}) %copy-start.1) | copy-done | bytes 536
  1.3 0.0 copy-start
  1.3 1.0 %copy-done = f32[128,1024]{1,0:T(8,128)S(1)} copy-done((f32[128,1024]{1,0:T(8,128)S(1)}, f32[128,1024]{1,0:T(8,128)}, u32[]{:S(2)}) %copy-start) | copy-done | bytes 524312
  2.3 52.5 %shard_map.50 = (f32[128,1024]{1,0:T(8,128)S(1)}, f32[128,1024]{1,0:T(8,128)S(1)}) custom-call(f32[128,1024]{1,0:T(8,128)S(1)} %copy-done, f32[128,1024]{1,0:T(8,128)} %p_hbm.1, s32[1,128]{1,0:T(1,128)S(1)} %bitcast.1), custom_call_target="tpu_custom_call" | custom-call | tf_op jit(solution)/shard_map/pallas_call | solution.py:509
  54.8 1.0 %shard_map.51 = (f32[128,1024]{1,0:T(8,128)}, f32[128,1024]{1,0:T(8,128)}) custom-call(f32[128,1024]{1,0:T(8,128)S(1)} %get-tuple-element.4.q_in, f32[128,1024]{1,0:T(8,128)S(1)} %get-tuple-element.5.p_in), custom_call_target="tpu_custom_call" | custom-call | tf_op jit(solution)/shard_map/pallas_call | solution.py:519
Async XLA Ops:
  0.6 0.7 %copy-start.1 = (s32[128]{0:T(128)S(1)}, s32[128]{0:T(128)}, u32[]{:S(2)}) copy-start(s32[128]{0:T(128)} %param.5) | copy-start | bytes 1540
  1.3 1.0 %copy-start = (f32[128,1024]{1,0:T(8,128)S(1)}, f32[128,1024]{1,0:T(8,128)}, u32[]{:S(2)}) copy-start(f32[128,1024]{1,0:T(8,128)} %q_hbm.1) | copy-start | bytes 1572868

commit v4 on v3

--- a/solution.py
+++ b/solution.py
@@ -75,7 +75,7 @@
     q_hbm, p_hbm, pos_in, q_out, p_out,
     qf, pf, q_len, p_len, qbuf, pbuf, pos_buf, e_ref, w_ref, racc, cacc,
     row_tx, row_rx, col_tx, col_rx, row_tot, col_tot, qpart, ppart, q_d2d, q_rx, p_rx,
-    shifted, row_inverse, local_sem, copy_sem,
+    row_inverse, local_sem, copy_sem,
 ):
     team, inner = lax.axis_index("team"), lax.axis_index("inner")
     x, c = team // 2, team % 2
@@ -94,6 +94,10 @@
 
     q_peers = [(r, s, t) for r in range(RING) for s in range(2) for t in range(2)][1:]
     p_peers = [(r, s) for r in range(RING) for s in range(2)][1:]
+
+    def far(peer):
+        return -min(peer[0], RING - peer[0]) - sum(peer[1:])
+
 
     loads = [
         pltpu.make_async_copy(q_hbm, qf, local_sem.at[0]),
@@ -182,10 +186,10 @@
         def fourth(self):
             self.take("xPB")
             self.take("yA1")
+            self.take("lPB2")
 
         def fifth(self):
             self.take("xB2")
-            self.take("lPB2")
             self.take("yA2")
 
     def share(name, place, half):
@@ -198,8 +202,8 @@
     pg.begin()
     send("c", qbuf.at[pl.ds(0, ROWS), :], qbuf.at[pl.ds(512, ROWS), :], sibling, "c", "c1")
 
-    def scores(rows0, rows1, cols0, cols1, step=512):
-        width = 256
+    def scores(rows0, rows1, cols0, cols1):
+        step = width = 256
         for i in range(rows0, rows1, step):
             rows = pl.ds(i, step)
             for j in range(cols0, cols1, width):
@@ -227,15 +231,15 @@
         g.second()
     scores(0, 512, 0, 512)
     landed("c1", 512, 512)
-    scores(512, 1024, 0, 512)
     for g in (qg, pg):
         g.third()
+    scores(512, 1024, 0, 512)
     for g in (qg, pg):
         g.fourth()
     scores(0, 1024, 512, 768)
-    scores(1024, 1280, 0, 768, 256)
+    scores(1024, 1280, 0, 768)
     landed("c2", 1280, 256)
-    scores(1280, 1536, 0, 768, 256)
+    scores(1280, 1536, 0, 768)
     for g in (qg, pg):
         g.fifth()
     blocks = [(place, t) for place in ORDER for t in range(2)]
@@ -243,9 +247,9 @@
         slot = q_row((-r % RING, s), t) // ROWS
         send(f"pos{r}{s}{t}", pos_buf.at[0], pos_buf.at[slot], q_device(r, s, t), "pos", "pos")
     scores(0, 1536, 768, 1024)
-    scores(1536, 1792, 0, 1024, 256)
+    scores(1536, 1792, 0, 1024)
     landed("c3", 1792, 256)
-    scores(1792, 2048, 0, 1024, 256)
+    scores(1792, 2048, 0, 1024)
 
     def q_index(r, s, t):
         yb = bit if s == 0 else 1 - bit
@@ -258,21 +262,31 @@
     for k, place in enumerate(ORDER):
         col = jnp.sum(cacc[:, pl.ds(k * ROWS, ROWS)], axis=0, keepdims=True)
         col_tx[pl.ds(p_index(*place), 1), :] = col
-    for r, s in p_peers:
+    for r, s in sorted(p_peers, key=far):
         slot = (-r % RING) * 2 + s
         send(f"col{r}{s}", col_tx, col_rx.at[slot], p_device(r, s), "col", "col")
     for place, t in blocks:
         turned = jnp.transpose(racc[pl.ds(q_row(place, t), ROWS), :])
         row_tx[pl.ds(q_index(*place, t), 1), :] = jnp.sum(turned, axis=0, keepdims=True)
-    for r, s, t in q_peers:
+    for r, s, t in sorted(q_peers, key=far):
         slot = (-r % RING) * 4 + s * 2 + t
         send(f"row{r}{s}{t}", row_tx, row_rx.at[slot], q_device(r, s, t), "row", "row")
+
+    def column_base(place):
+        r, s = place
+        zz, yy = (z + r) % RING, y if s == 0 else 3 - y
+        return (team * 16 + zz * RING + yy) * ROWS
+
+    bases = [column_base(place).astype(F32) for place in ORDER]
 
     links.all_arrived("pos", pos_buf.at[pl.ds(1, 15)])
     lane = lax.broadcasted_iota(jnp.int32, (ROWS, 128), 1).astype(F32)
     for k in range(16):
         target = jnp.broadcast_to(pos_buf[k, pl.ds(0, 1), :].astype(F32), (128, 128))
-        shifted[pl.ds(k * ROWS, ROWS), :] = jnp.transpose(target) - lane
+        shifted = jnp.transpose(target) - lane
+        for j in range(8):
+            hit = jnp.where(shifted == bases[j], -2.0, 0.0)
+            w_ref[pl.ds(k * ROWS, ROWS), pl.ds(j * 128, 128)] = hit.astype(BF16)
     links.all_arrived("col", col_rx.at[pl.ds(1, 7)])
     total = col_tx[...]
     for i in range(1, 8):
@@ -289,26 +303,21 @@
     for k, place in enumerate(ORDER):
         col_tot[pl.ds(8 + k, 1), :] = col_tot[pl.ds(p_index(*place), 1), :]
 
-    def column_base(place):
-        r, s = place
-        zz, yy = (z + r) % RING, y if s == 0 else 3 - y
-        return (team * 16 + zz * RING + yy) * ROWS
-
-    bases = [column_base(place).astype(F32) for place in ORDER]
-
     def row_factor(k):
         rows = pl.ds(k * ROWS, ROWS)
         factor = jnp.broadcast_to(row_tot[pl.ds(16 + k, 1), :], (128, 128))
         row_inverse[rows, :] = jnp.transpose(factor)
 
-    def weight(k, j):
-        rows, cols = pl.ds(k * ROWS, ROWS), pl.ds(j * 128, 128)
-        w = e_ref[rows, cols] * (row_inverse[rows, :] + col_tot[pl.ds(8 + j, 1), :])
-        w = w - jnp.where(shifted[rows, :] == bases[j], 2.0, 0.0)
-        w_ref[rows, cols] = w.astype(BF16)
-
-    def weights(slots, cols):
-        return [(weight, k, j) for k in slots for j in cols]
+    def weight(k, columns):
+        rows = pl.ds(k * ROWS, ROWS)
+        factor = row_inverse[rows, :]
+        for j in columns:
+            cols = pl.ds(j * 128, 128)
+            w = e_ref[rows, cols] * (factor + col_tot[pl.ds(8 + j, 1), :])
+            w_ref[rows, cols] += w.astype(BF16)
+
+    def weights(slots, columns):
+        return [(weight, k, columns) for k in slots]
 
     def run(work):
         for f, *args in work:
@@ -323,22 +332,18 @@
             ).astype(BF16)
             run(beside[len(beside) * i // 4 : len(beside) * (i + 1) // 4])
 
-    def q_dots(own, other, blocks, shared_first, beside=()):
-        half = len(beside) // 2
-        rows = blocks * ROWS
-        q_dot(other, other + rows, beside[:half])
+    def to_sibling(first, rows, place_row):
         send(
-            f"d{shared_first}",
-            qpart.at[pl.ds(other, rows), :],
-            q_d2d.at[pl.ds(shared_first, rows), :],
+            f"d{place_row}",
+            qpart.at[pl.ds(first, rows), :],
+            q_d2d.at[pl.ds(place_row, rows), :],
             sibling,
             "d",
         )
-        q_dot(own, own + rows, beside[half:])
-
-    def p_dot(first, last, tiles=range(4), beside=()):
+
+    def p_dot(first, last, beside=()):
         out = pl.ds(first, last - first)
-        for n, i in enumerate(tiles):
+        for i in range(4):
             cols = pl.ds(i * 256, 256)
             ppart[out, cols] = lax.dot_general(
                 w_ref[:, out],
@@ -346,7 +351,7 @@
                 (((0,), (0,)), ((), ())),
                 preferred_element_type=F32,
             ).astype(BF16)
-            run(beside[len(beside) * n // len(tiles) : len(beside) * (n + 1) // len(tiles)])
+            run(beside[len(beside) * i // 4 : len(beside) * (i + 1) // 4])
 
     class Reduce:
         def __init__(self, tag, part, row, extra, rx, right, left, pair):
@@ -421,37 +426,41 @@
         row_factor(k)
     run(weights(range(12, 16), range(8)))
     later = [(row_factor, k) for k in range(12)] + weights(range(12), (6, 7))
-    q_dots(1536, 1792, 2, 768, later)
-    later = weights(range(8, 12), range(6))
-    p_dot(768, 1024, (0, 1), later[:12])
+    q_dot(1792, 2048, later)
+    to_sibling(1792, 256, 768)
+    p_dot(768, 1024, weights(range(12), (4, 5)))
+    pr.one()
+    q_dot(1536, 1792, weights(range(8, 12), range(4)))
     arrived("d768")
     qr.one()
-    p_dot(768, 1024, (2, 3), later[12:])
-    pr.one()
-    q_dots(1024, 1280, 2, 512, weights(range(8), (4, 5)))
     later = weights(range(8), range(4))
-    p_dot(512, 768, (0, 1), later[:16])
+    q_dot(1280, 1536, later[:2])
+    to_sibling(1280, 256, 512)
+    p_dot(512, 768, later[2:6])
+    pr.two()
+    q_dot(1024, 1280, later[6:])
     arrived("d512")
     qr.two()
-    p_dot(512, 768, (2, 3), later[16:])
-    pr.two()
+    p_dot(128, 512)
+    pr.three()
+    pr.four()
     qr.three()
-    q_dots(128, 640, 3, 128)
-    pr.three()
-    p_dot(128, 512, (0, 1))
+    q_dot(640, 1024)
+    to_sibling(640, 384, 128)
+    q_dot(128, 512)
+    q_dot(512, 640)
+    to_sibling(512, 128, 0)
+    q_dot(0, 128)
     arrived("d128")
     qr.four()
-    p_dot(128, 512, (2, 3))
-    pr.four()
+    pr.five()
+    p_dot(0, 128)
+    pr.six()
     qr.five()
-    q_dots(0, 512, 1, 0)
     qr.six()
-    p_dot(0, 128)
-    pr.five()
-    pr.six()
     arrived("d0")
+    pr.finish(pf, p_len, p_out)
     qr.finish(qf, q_len, q_out)
-    pr.finish(pf, p_len, p_out)
     for sent, like in (
         ("q", q_rx), ("p", p_rx), ("Q", q_rx), ("P", p_rx),
         ("c", q_d2d), ("d", q_d2d),
@@ -499,7 +508,6 @@
         vmem((14, HALF, D), BF16),
         vmem((14, HALF, D), BF16),
         vmem((NQ, 128), F32),
-        vmem((NQ, 128), F32),
         pltpu.SemaphoreType.DMA((2,)),
         pltpu.SemaphoreType.DMA((SEMAPHORES,)),
     ]

time: 56.6 us -> 57.4 us (1.014)
  Pallas kernels: 53.5 us -> 54.7 us
    pallas_call x1, Pallas kernels: 52.5 us -> 53.7 us  [per_device(): pl.pallas_call(kernel, out_shape=(out, out), in_specs=[hbm, hbm, here], o...]
where the time goes in v4:
time: 57.4 us; the launch traced here: 57.2 us
  Pallas kernels  54.7 us (95%)
  local copies, waits for them, and re-layouts  1.69 us (3%)
  between operations  0.81 us (1%)
    pallas_call x1, Pallas kernels, per_device(): pl.pallas_call(kernel, out_shape=(out, out), in_specs=[hbm, hbm, here], o...  53.7 us
    unnamed x4, local copies, waits for them, and re-layouts  1.69 us

profile of v4, /device:TPU:0, one launch (start us, length us, event | category | flops | bytes accessed | tf_op | source)
XLA Modules:
  0.0 57.2 jit_solution(15876660741940037272)
XLA Ops:
  0.6 0.0 copy-start.1
  0.6 0.6 %copy-done.1 = s32[128]{0:T(128)S(1)} copy-done((s32[128]{0:T(128)S(1)}, s32[128]{0:T(128)}, u32[]{:S(2)}) %copy-start.1) | copy-done | bytes 536
  1.3 0.0 copy-start
  1.3 1.0 %copy-done = f32[128,1024]{1,0:T(8,128)S(1)} copy-done((f32[128,1024]{1,0:T(8,128)S(1)}, f32[128,1024]{1,0:T(8,128)}, u32[]{:S(2)}) %copy-start) | copy-done | bytes 524312
  2.3 53.7 %shard_map.50 = (f32[128,1024]{1,0:T(8,128)S(1)}, f32[128,1024]{1,0:T(8,128)S(1)}) custom-call(f32[128,1024]{1,0:T(8,128)S(1)} %copy-done, f32[128,1024]{1,0:T(8,128)} %p_hbm.1, s32[1,128]{1,0:T(1,128)S(1)} %bitcast.1), custom_call_target="tpu_custom_call" | custom-call | tf_op jit(solution)/shard_map/pallas_call | solution.py:517
  56.1 1.0 %shard_map.51 = (f32[128,1024]{1,0:T(8,128)}, f32[128,1024]{1,0:T(8,128)}) custom-call(f32[128,1024]{1,0:T(8,128)S(1)} %get-tuple-element.4.q_in, f32[128,1024]{1,0:T(8,128)S(1)} %get-tuple-element.5.p_in), custom_call_target="tpu_custom_call" | custom-call | tf_op jit(solution)/shard_map/pallas_call | solution.py:527
Async XLA Ops:
  0.6 0.7 %copy-start.1 = (s32[128]{0:T(128)S(1)}, s32[128]{0:T(128)}, u32[]{:S(2)}) copy-start(s32[128]{0:T(128)} %param.5) | copy-start | bytes 1540
  1.3 1.0 %copy-start = (f32[128,1024]{1,0:T(8,128)S(1)}, f32[128,1024]{1,0:T(8,128)}, u32[]{:S(2)}) copy-start(f32[128,1024]{1,0:T(8,128)} %q_hbm.1) | copy-start | bytes 1572868

commit v5 on v4

--- a/solution.py
+++ b/solution.py
@@ -186,7 +186,6 @@
         def fourth(self):
             self.take("xPB")
             self.take("yA1")
-            self.take("lPB2")
 
         def fifth(self):
             self.take("xB2")
@@ -222,6 +221,15 @@
                 racc[rows, :] += part
                 cacc[:, cols] += jnp.sum(e.reshape(step // 8, 8, width), axis=0)
 
+    def q_index(r, s, t):
+        yb = bit if s == 0 else 1 - bit
+        return ((x + r) % RING) * 4 + yb * 2 + (c if t == 0 else 1 - c)
+
+    def sum_rows(blocks):
+        for place, t in blocks:
+            turned = jnp.transpose(racc[pl.ds(q_row(place, t), ROWS), :])
+            row_tx[pl.ds(q_index(*place, t), 1), :] = jnp.sum(turned, axis=0, keepdims=True)
+
     def landed(stage, rows, count):
         links.all_arrived(stage, qbuf.at[pl.ds(rows, count), :])
 
@@ -238,22 +246,21 @@
         g.fourth()
     scores(0, 1024, 512, 768)
     scores(1024, 1280, 0, 768)
+    for g in (qg, pg):
+        g.take("lPB2")
     landed("c2", 1280, 256)
     scores(1280, 1536, 0, 768)
     for g in (qg, pg):
         g.fifth()
-    blocks = [(place, t) for place in ORDER for t in range(2)]
+    blocks = sorted(((place, t) for place in ORDER for t in range(2)), key=lambda b: q_row(*b))
     for r, s, t in q_peers:
         slot = q_row((-r % RING, s), t) // ROWS
         send(f"pos{r}{s}{t}", pos_buf.at[0], pos_buf.at[slot], q_device(r, s, t), "pos", "pos")
     scores(0, 1536, 768, 1024)
     scores(1536, 1792, 0, 1024)
+    sum_rows(blocks[:-2])
     landed("c3", 1792, 256)
     scores(1792, 2048, 0, 1024)
-
-    def q_index(r, s, t):
-        yb = bit if s == 0 else 1 - bit
-        return ((x + r) % RING) * 4 + yb * 2 + (c if t == 0 else 1 - c)
 
     def p_index(r, s):
         yb = bit if s == 0 else 1 - bit
@@ -265,9 +272,7 @@
     for r, s in sorted(p_peers, key=far):
         slot = (-r % RING) * 2 + s
         send(f"col{r}{s}", col_tx, col_rx.at[slot], p_device(r, s), "col", "col")
-    for place, t in blocks:
-        turned = jnp.transpose(racc[pl.ds(q_row(place, t), ROWS), :])
-        row_tx[pl.ds(q_index(*place, t), 1), :] = jnp.sum(turned, axis=0, keepdims=True)
+    sum_rows(blocks[-2:])
     for r, s, t in sorted(q_peers, key=far):
         slot = (-r % RING) * 4 + s * 2 + t
         send(f"row{r}{s}{t}", row_tx, row_rx.at[slot], q_device(r, s, t), "row", "row")

time: 57.4 us -> 56.2 us (0.979)
  Pallas kernels: 54.7 us -> 53.5 us
    pallas_call x1, Pallas kernels: 53.7 us -> 52.5 us  [per_device(): pl.pallas_call(kernel, out_shape=(out, out), in_specs=[hbm, hbm, here], o...]
where the time goes in v5:
time: 56.2 us; the launch traced here: 56 us
  Pallas kernels  53.5 us (95%)
  local copies, waits for them, and re-layouts  1.69 us (3%)
  between operations  0.81 us (1%)
    pallas_call x1, Pallas kernels, per_device(): pl.pallas_call(kernel, out_shape=(out, out), in_specs=[hbm, hbm, here], o...  52.5 us
    unnamed x4, local copies, waits for them, and re-layouts  1.69 us

profile of v5, /device:TPU:0, one launch (start us, length us, event | category | flops | bytes accessed | tf_op | source)
XLA Modules:
  0.0 56.0 jit_solution(6624078706142981045)
XLA Ops:
  0.6 0.0 copy-start.1
  0.6 0.6 %copy-done.1 = s32[128]{0:T(128)S(1)} copy-done((s32[128]{0:T(128)S(1)}, s32[128]{0:T(128)}, u32[]{:S(2)}) %copy-start.1) | copy-done | bytes 536
  1.3 0.0 copy-start
  1.3 1.0 %copy-done = f32[128,1024]{1,0:T(8,128)S(1)} copy-done((f32[128,1024]{1,0:T(8,128)S(1)}, f32[128,1024]{1,0:T(8,128)}, u32[]{:S(2)}) %copy-start) | copy-done | bytes 524312
  2.3 52.5 %shard_map.50 = (f32[128,1024]{1,0:T(8,128)S(1)}, f32[128,1024]{1,0:T(8,128)S(1)}) custom-call(f32[128,1024]{1,0:T(8,128)S(1)} %copy-done, f32[128,1024]{1,0:T(8,128)} %p_hbm.1, s32[1,128]{1,0:T(1,128)S(1)} %bitcast.1), custom_call_target="tpu_custom_call" | custom-call | tf_op jit(solution)/shard_map/pallas_call | solution.py:522
  54.8 1.0 %shard_map.51 = (f32[128,1024]{1,0:T(8,128)}, f32[128,1024]{1,0:T(8,128)}) custom-call(f32[128,1024]{1,0:T(8,128)S(1)} %get-tuple-element.4.q_in, f32[128,1024]{1,0:T(8,128)S(1)} %get-tuple-element.5.p_in), custom_call_target="tpu_custom_call" | custom-call | tf_op jit(solution)/shard_map/pallas_call | solution.py:532
Async XLA Ops:
  0.6 0.7 %copy-start.1 = (s32[128]{0:T(128)S(1)}, s32[128]{0:T(128)}, u32[]{:S(2)}) copy-start(s32[128]{0:T(128)} %param.5) | copy-start | bytes 1540
  1.3 1.0 %copy-start = (f32[128,1024]{1,0:T(8,128)S(1)}, f32[128,1024]{1,0:T(8,128)}, u32[]{:S(2)}) copy-start(f32[128,1024]{1,0:T(8,128)} %q_hbm.1) | copy-start | bytes 1572868

commit v6 on v5

--- a/solution.py
+++ b/solution.py
@@ -72,8 +72,8 @@
 
 
 def kernel(
-    q_hbm, p_hbm, pos_in, q_out, p_out,
-    qf, pf, q_len, p_len, qbuf, pbuf, pos_buf, e_ref, w_ref, racc, cacc,
+    q_hbm, p_hbm, pos_hbm, q_out, p_out,
+    qf, pf, pos_in, q_len, p_len, qbuf, pbuf, pos_buf, e_ref, w_ref, racc, cacc,
     row_tx, row_rx, col_tx, col_rx, row_tot, col_tot, qpart, ppart, q_d2d, q_rx, p_rx,
     row_inverse, local_sem, copy_sem,
 ):
@@ -102,6 +102,7 @@
     loads = [
         pltpu.make_async_copy(q_hbm, qf, local_sem.at[0]),
         pltpu.make_async_copy(p_hbm, pf, local_sem.at[1]),
+        pltpu.make_async_copy(pos_hbm, pos_in, local_sem.at[2]),
     ]
     for load in loads:
         load.start()
@@ -127,9 +128,6 @@
     normalize(qf, q_len, qbuf)
     loads[1].wait()
     normalize(pf, p_len, pbuf)
-    pos_buf[0] = jnp.broadcast_to(pos_in[...], (8, 128))
-    racc[...] = jnp.zeros_like(racc)
-    cacc[...] = jnp.zeros_like(cacc)
     pl.semaphore_wait(barrier, len(neighbours))
 
     def q_at(place, half, t=0):
@@ -200,6 +198,10 @@
     qg.begin()
     pg.begin()
     send("c", qbuf.at[pl.ds(0, ROWS), :], qbuf.at[pl.ds(512, ROWS), :], sibling, "c", "c1")
+    loads[2].wait()
+    pos_buf[0] = jnp.broadcast_to(pos_in[...], (8, 128))
+    racc[...] = jnp.zeros_like(racc)
+    cacc[...] = jnp.zeros_like(cacc)
 
     def scores(rows0, rows1, cols0, cols1):
         step = width = 256
@@ -492,6 +494,7 @@
     scratch = [
         vmem((ROWS, D), F32),
         vmem((ROWS, D), F32),
+        vmem((1, ROWS), jnp.int32),
         vmem((ROWS, 128), F32),
         vmem((ROWS, 128), F32),
         vmem((NQ, D), BF16),
@@ -513,7 +516,7 @@
         vmem((14, HALF, D), BF16),
         vmem((14, HALF, D), BF16),
         vmem((NQ, 128), F32),
-        pltpu.SemaphoreType.DMA((2,)),
+        pltpu.SemaphoreType.DMA((3,)),
         pltpu.SemaphoreType.DMA((SEMAPHORES,)),
     ]
     out = jax.ShapeDtypeStruct((ROWS, D), F32)
@@ -522,13 +525,17 @@
     grads = pl.pallas_call(
         kernel,
         out_shape=(out, out),
-        in_specs=[hbm, hbm, here],
+        in_specs=[hbm, hbm, hbm],
         out_specs=(here, here),
         scratch_shapes=scratch,
         compiler_params=pltpu.CompilerParams(
             collective_id=0, has_side_effects=True, vmem_limit_bytes=52 << 20
         ),
-    )(queries, passages, positive.reshape(1, ROWS))
+    )(
+        pltpu.with_memory_space_constraint(queries, pltpu.HBM),
+        pltpu.with_memory_space_constraint(passages, pltpu.HBM),
+        pltpu.with_memory_space_constraint(positive.reshape(1, ROWS), pltpu.HBM),
+    )
     return pl.pallas_call(
         put_out,
         out_shape=(out, out),

time: 56.2 us -> 54.5 us (0.970)
  local copies, waits for them, and re-layouts: 1.69 us -> 0 us
    unnamed x4 -> x0, local copies, waits for them, and re-layouts: 1.69 us -> none
where the time goes in v6:
time: 54.5 us; the launch traced here: 54.3 us
  Pallas kernels  53.5 us (98%)
  between operations  0.8 us (1%)
    pallas_call x1, Pallas kernels, per_device(): pl.pallas_call(kernel, out_shape=(out, out), in_specs=[hbm, hbm, hbm], ou...  52.6 us

profile of v6, /device:TPU:0, one launch (start us, length us, event | category | flops | bytes accessed | tf_op | source)
XLA Modules:
  0.0 54.3 jit_solution(17495790115764732551)
XLA Ops:
  0.6 52.6 %shard_map.50 = (f32[128,1024]{1,0:T(8,128)S(1)}, f32[128,1024]{1,0:T(8,128)S(1)}) custom-call(f32[128,1024]{1,0:T(8,128)} %q_hbm.1, f32[128,1024]{1,0:T(8,128)} %p_hbm.1, s32[1,128]{1,0:T(1,128)} %bitcast.1), custom_call_target="tpu_custom_call" | custom-call | tf_op jit(solution)/shard_map/pallas_call | solution.py:525
  53.2 1.0 %shard_map.51 = (f32[128,1024]{1,0:T(8,128)}, f32[128,1024]{1,0:T(8,128)}) custom-call(f32[128,1024]{1,0:T(8,128)S(1)} %get-tuple-element.4.q_in, f32[128,1024]{1,0:T(8,128)S(1)} %get-tuple-element.5.p_in), custom_call_target="tpu_custom_call" | custom-call | tf_op jit(solution)/shard_map/pallas_call | solution.py:539

commit v7 on v6

--- a/solution.py
+++ b/solution.py
@@ -73,7 +73,7 @@
 
 def kernel(
     q_hbm, p_hbm, pos_hbm, q_out, p_out,
-    qf, pf, pos_in, q_len, p_len, qbuf, pbuf, pos_buf, e_ref, w_ref, racc, cacc,
+    qf, pf, pos_in, q_inverse, p_inverse, qbuf, pbuf, pos_buf, e_ref, w_ref, racc, cacc,
     row_tx, row_rx, col_tx, col_rx, row_tot, col_tot, qpart, ppart, q_d2d, q_rx, p_rx,
     row_inverse, local_sem, copy_sem,
 ):
@@ -116,18 +116,18 @@
     links = Links(copy_sem, sibling)
     send, arrived = links.send, links.arrived
 
-    def normalize(full, length_ref, rounded):
+    def normalize(full, inverse_ref, rounded):
         v = full[...]
-        length = jnp.sqrt(jnp.sum(v * v, axis=1, keepdims=True) + EPSILON)
-        unit = v / length
+        inverse = 1.0 / jnp.sqrt(jnp.sum(v * v, axis=1, keepdims=True) + EPSILON)
+        unit = v * inverse
         full[...] = unit
-        length_ref[...] = jnp.broadcast_to(length, (ROWS, 128))
+        inverse_ref[...] = jnp.broadcast_to(inverse, (ROWS, 128))
         rounded[pl.ds(0, ROWS), :] = unit.astype(BF16)
 
     loads[0].wait()
-    normalize(qf, q_len, qbuf)
+    normalize(qf, q_inverse, qbuf)
     loads[1].wait()
-    normalize(pf, p_len, pbuf)
+    normalize(pf, p_inverse, pbuf)
     pl.semaphore_wait(barrier, len(neighbours))
 
     def q_at(place, half, t=0):
@@ -412,13 +412,13 @@
             self.send("lAl", (3, 0), A, "yA3")
             self.send("xAr", (1, 0), A, "yA1", "xAo")
 
-        def finish(self, unit_ref, length_ref, out_ref):
+        def finish(self, unit_ref, inverse_ref, out_ref):
             for half, names in ((B, ("xB0r", "lB0l", "yB1f")), (A, ("yA0", "lAl", "xAr"))):
                 rows = pl.ds(half * HALF, HALF)
                 raw = self.total((0, 0), half, names) * SCALE
                 unit = unit_ref[rows, :]
                 along = jnp.sum(unit * raw, axis=1, keepdims=True)
-                out_ref[rows, :] = (raw - unit * along) / length_ref[rows, 0:1]
+                out_ref[rows, :] = (raw - unit * along) * inverse_ref[rows, 0:1]
 
     qr = Reduce(
         "Q", qpart, lambda place: q_row(place, 0), q_d2d, q_rx,
@@ -466,8 +466,8 @@
     qr.five()
     qr.six()
     arrived("d0")
-    pr.finish(pf, p_len, p_out)
-    qr.finish(qf, q_len, q_out)
+    pr.finish(pf, p_inverse, p_out)
+    qr.finish(qf, q_inverse, q_out)
     for sent, like in (
         ("q", q_rx), ("p", p_rx), ("Q", q_rx), ("P", p_rx),
         ("c", q_d2d), ("d", q_d2d),

time: 54.5 us -> 54.5 us (level)
  no operation moved by 1% of the time
where the time goes in v7:
time: 54.5 us; the launch traced here: 54.3 us
  Pallas kernels  53.5 us (98%)
  between operations  0.8 us (1%)
    pallas_call x1, Pallas kernels, per_device(): pl.pallas_call(kernel, out_shape=(out, out), in_specs=[hbm, hbm, hbm], ou...  52.5 us

profile of v7, /device:TPU:0, one launch (start us, length us, event | category | flops | bytes accessed | tf_op | source)
XLA Modules:
  0.0 54.3 jit_solution(9619027446103075048)
XLA Ops:
  0.6 52.5 %shard_map.50 = (f32[128,1024]{1,0:T(8,128)S(1)}, f32[128,1024]{1,0:T(8,128)S(1)}) custom-call(f32[128,1024]{1,0:T(8,128)} %q_hbm.1, f32[128,1024]{1,0:T(8,128)} %p_hbm.1, s32[1,128]{1,0:T(1,128)} %bitcast.1), custom_call_target="tpu_custom_call" | custom-call | tf_op jit(solution)/shard_map/pallas_call | solution.py:525
  53.2 1.0 %shard_map.51 = (f32[128,1024]{1,0:T(8,128)}, f32[128,1024]{1,0:T(8,128)}) custom-call(f32[128,1024]{1,0:T(8,128)S(1)} %get-tuple-element.4.q_in, f32[128,1024]{1,0:T(8,128)S(1)} %get-tuple-element.5.p_in), custom_call_target="tpu_custom_call" | custom-call | tf_op jit(solution)/shard_map/pallas_call | solution.py:539

commit v8 on v7

--- a/solution.py
+++ b/solution.py
@@ -435,17 +435,17 @@
     later = [(row_factor, k) for k in range(12)] + weights(range(12), (6, 7))
     q_dot(1792, 2048, later)
     to_sibling(1792, 256, 768)
-    p_dot(768, 1024, weights(range(12), (4, 5)))
+    p_dot(768, 1024)
     pr.one()
-    q_dot(1536, 1792, weights(range(8, 12), range(4)))
+    q_dot(1536, 1792, weights(range(8, 12), range(6)))
     arrived("d768")
     qr.one()
     later = weights(range(8), range(4))
-    q_dot(1280, 1536, later[:2])
+    q_dot(1280, 1536, weights(range(8), (4, 5)))
     to_sibling(1280, 256, 512)
-    p_dot(512, 768, later[2:6])
+    p_dot(512, 768, later[:4])
     pr.two()
-    q_dot(1024, 1280, later[6:])
+    q_dot(1024, 1280, later[4:])
     arrived("d512")
     qr.two()
     p_dot(128, 512)

time: 54.5 us -> 54.4 us (level)
  no operation moved by 1% of the time
where the time goes in v8:
time: 54.4 us; the launch traced here: 54.3 us
  Pallas kernels  53.5 us (98%)
  between operations  0.8 us (1%)
    pallas_call x1, Pallas kernels, per_device(): pl.pallas_call(kernel, out_shape=(out, out), in_specs=[hbm, hbm, hbm], ou...  52.5 us

profile of v8, /device:TPU:0, one launch (start us, length us, event | category | flops | bytes accessed | tf_op | source)
XLA Modules:
  0.0 54.3 jit_solution(12138981906057222675)
XLA Ops:
  0.6 52.5 %shard_map.50 = (f32[128,1024]{1,0:T(8,128)S(1)}, f32[128,1024]{1,0:T(8,128)S(1)}) custom-call(f32[128,1024]{1,0:T(8,128)} %q_hbm.1, f32[128,1024]{1,0:T(8,128)} %p_hbm.1, s32[1,128]{1,0:T(1,128)} %bitcast.1), custom_call_target="tpu_custom_call" | custom-call | tf_op jit(solution)/shard_map/pallas_call | solution.py:525
  53.2 1.0 %shard_map.51 = (f32[128,1024]{1,0:T(8,128)}, f32[128,1024]{1,0:T(8,128)}) custom-call(f32[128,1024]{1,0:T(8,128)S(1)} %get-tuple-element.4.q_in, f32[128,1024]{1,0:T(8,128)S(1)} %get-tuple-element.5.p_in), custom_call_target="tpu_custom_call" | custom-call | tf_op jit(solution)/shard_map/pallas_call | solution.py:539
